TPU v7x, 32 devices: a 4x4x1 block of a 4x4x8 slice. The times are simulated.
32 devices in a mesh: dp: 1 (over z), cp: 32 (over y, x, core).
Axes of the slice: x: 4, y: 4, z: 1, core: 2. Of those that a mesh axis runs over, the one named last changes fastest.
The devices are a block of a 4x4x8 slice.
Arguments:
- x_a: bfloat16 [512, 4096], P(('dp', 'cp'))
- kc_a: bfloat16 [16384, 8, 128], P(('dp', 'cp'))
- vc_a: bfloat16 [16384, 8, 128], P(('dp', 'cp'))
- x_b: bfloat16 [8192, 4096], P(('dp', 'cp'))
- kc_b: bfloat16 [4096, 8, 128], P(('dp', 'cp'))
- vc_b: bfloat16 [4096, 8, 128], P(('dp', 'cp'))
- w_q: bfloat16 [4096, 4096], replicated
- w_k: bfloat16 [4096, 1024], replicated
- w_v: bfloat16 [4096, 1024], replicated
- w_o: bfloat16 [4096, 4096], replicated
Outputs:
- output 1: bfloat16 [512, 4096], P(('dp', 'cp'))
- output 2: bfloat16 [512, 8, 128], P(('dp', 'cp'))
- output 3: bfloat16 [512, 8, 128], P(('dp', 'cp'))
- output 4: bfloat16 [8192, 4096], P(('dp', 'cp'))
- output 5: bfloat16 [8192, 8, 128], P(('dp', 'cp'))
- output 6: bfloat16 [8192, 8, 128], P(('dp', 'cp'))
All inputs are finite; a program needn't handle non-finite values.
Results may differ from a plain program's by a relative error of at most 0.0175995.
Values are sent between devices in bfloat16 or wider.
A program may use at most 768 MiB of HBM per device.

v0:
```python
import jax
import jax.numpy as jnp
from jax import lax
from jax.sharding import PartitionSpec as P

ROPE_BASE = 500000
MASK_FILL = -1e30


def rotary(heads_x, positions):
    head_dim = heads_x.shape[-1]
    half_dim = head_dim // 2
    inv_freq = jnp.power(jnp.float32(ROPE_BASE), jnp.arange(half_dim, dtype=jnp.float32) * (-2.0 / head_dim))
    angles = positions.astype(jnp.float32)[:, None] * inv_freq[None, :]
    bshape = (positions.shape[0],) + (1,) * (heads_x.ndim - 2) + (half_dim,)
    cos_ang = jnp.cos(angles).reshape(bshape)
    sin_ang = jnp.sin(angles).reshape(bshape)
    x_f32 = heads_x.astype(jnp.float32)
    x_first = x_f32[..., :half_dim]
    x_second = x_f32[..., half_dim:]
    rotated = jnp.concatenate([x_first * cos_ang - x_second * sin_ang, x_second * cos_ang + x_first * sin_ang], axis=-1)
    return rotated.astype(jnp.bfloat16)


def project(tok_rows, w_q, w_k, w_v, positions, kv_heads, head_dim):
    n_tok = tok_rows.shape[0]
    q_lin = jnp.dot(tok_rows, w_q, preferred_element_type=jnp.float32).astype(jnp.bfloat16)
    k_lin = jnp.dot(tok_rows, w_k, preferred_element_type=jnp.float32).astype(jnp.bfloat16)
    v_lin = jnp.dot(tok_rows, w_v, preferred_element_type=jnp.float32).astype(jnp.bfloat16)
    q_grp = rotary(q_lin.reshape(n_tok, kv_heads, -1, head_dim), positions)
    k_new = rotary(k_lin.reshape(n_tok, kv_heads, head_dim), positions)
    return q_grp, k_new, v_lin.reshape(n_tok, kv_heads, head_dim)


def block_attend(q_grp, blk_keys, blk_vals, allowed):
    attn_scale = q_grp.shape[-1] ** -0.5
    scores = jnp.einsum("tkgd,skd->tkgs", q_grp, blk_keys, preferred_element_type=jnp.float32) * attn_scale
    if allowed is not None:
        scores = jnp.where(allowed[:, None, None, :], scores, MASK_FILL)
    row_max = jnp.max(scores, axis=-1, keepdims=True)
    exp_s = jnp.exp(scores - row_max)
    if allowed is not None:
        exp_s = jnp.where(allowed[:, None, None, :], exp_s, 0.0)
    row_sum = jnp.sum(exp_s, axis=-1)
    pv_sum = jnp.einsum("tkgs,skd->tkgd", exp_s.astype(jnp.bfloat16), blk_vals, preferred_element_type=jnp.float32)
    part_o = pv_sum / jnp.maximum(row_sum, 1e-30)[..., None]
    part_lse = row_max[..., 0] + jnp.log(row_sum)
    return part_o, part_lse


def merge_parts(o_a, lse_a, o_b, lse_b):
    lse_new = jnp.logaddexp(lse_a, lse_b)
    o_new = o_a * jnp.exp(lse_a - lse_new)[..., None] + o_b * jnp.exp(lse_b - lse_new)[..., None]
    return o_new, lse_new


def attend_blocks(q_grp, blocks_k, blocks_v, q_pos):
    num_blocks = blocks_k.shape[0]
    blk_len = blocks_k.shape[1]
    local_pos = jnp.arange(blk_len)

    def mask_for(blk_idx):
        if q_pos is None:
            return None
        return (blk_idx * blk_len + local_pos)[None, :] <= q_pos[:, None]

    first_o, first_lse = block_attend(q_grp, blocks_k[0], blocks_v[0], mask_for(0))

    def visit(blk_idx, loop_carry):
        blk_keys = lax.dynamic_index_in_dim(blocks_k, blk_idx, 0, keepdims=False)
        blk_vals = lax.dynamic_index_in_dim(blocks_v, blk_idx, 0, keepdims=False)
        part_o, part_lse = block_attend(q_grp, blk_keys, blk_vals, mask_for(blk_idx))
        return merge_parts(loop_carry[0], loop_carry[1], part_o, part_lse)

    return lax.fori_loop(1, num_blocks, visit, (first_o, first_lse))


def solution(mesh):
    cp_size = mesh.shape["cp"]
    next_perm = [(src_dev, (src_dev + 1) % cp_size) for src_dev in range(cp_size)]

    def queries_to_cache(q_grp, cache_k, cache_v):
        first_o, first_lse = block_attend(q_grp, cache_k, cache_v, None)

        def visit(step_idx, loop_carry):
            q_cur = lax.ppermute(loop_carry[0], "cp", next_perm)
            acc_o = lax.ppermute(loop_carry[1], "cp", next_perm)
            acc_lse = lax.ppermute(loop_carry[2], "cp", next_perm)
            part_o, part_lse = block_attend(q_cur, cache_k, cache_v, None)
            acc_o, acc_lse = merge_parts(acc_o, acc_lse, part_o, part_lse)
            return q_cur, acc_o, acc_lse

        loop_carry = lax.fori_loop(1, cp_size, visit, (q_grp, first_o, first_lse))
        return lax.ppermute(loop_carry[1], "cp", next_perm), lax.ppermute(loop_carry[2], "cp", next_perm)

    def cache_to_queries(q_grp, cache_k, cache_v):
        first_o, first_lse = block_attend(q_grp, cache_k, cache_v, None)

        def visit(step_idx, loop_carry):
            blk_keys = lax.ppermute(loop_carry[0], "cp", next_perm)
            blk_vals = lax.ppermute(loop_carry[1], "cp", next_perm)
            part_o, part_lse = block_attend(q_grp, blk_keys, blk_vals, None)
            acc_o, acc_lse = merge_parts(loop_carry[2], loop_carry[3], part_o, part_lse)
            return blk_keys, blk_vals, acc_o, acc_lse

        loop_carry = lax.fori_loop(1, cp_size, visit, (cache_k, cache_v, first_o, first_lse))
        return loop_carry[2], loop_carry[3]

    def request(tok_rows, cache_k, cache_v, w_q, w_k, w_v, w_o, use_queries):
        n_tok = tok_rows.shape[0]
        kv_heads = cache_k.shape[1]
        head_dim = cache_k.shape[2]
        local_pos = lax.axis_index("cp") * n_tok + jnp.arange(n_tok)
        q_grp, k_new, v_new = project(tok_rows, w_q, w_k, w_v, cache_k.shape[0] * cp_size + local_pos, kv_heads, head_dim)
        own_o, own_lse = attend_blocks(q_grp, lax.all_gather(k_new, "cp"), lax.all_gather(v_new, "cp"), local_pos)
        if use_queries:
            far_o, far_lse = queries_to_cache(q_grp, cache_k, cache_v)
        else:
            far_o, far_lse = cache_to_queries(q_grp, cache_k, cache_v)
        acc_o = merge_parts(own_o, own_lse, far_o, far_lse)[0]
        attn_out = acc_o.reshape(n_tok, -1).astype(jnp.bfloat16)
        y_out = jnp.dot(attn_out, w_o, preferred_element_type=jnp.float32).astype(jnp.bfloat16)
        return y_out, k_new, v_new

    def local_step(x_a, kc_a, vc_a, x_b, kc_b, vc_b, w_q, w_k, w_v, w_o):
        out_a = request(x_a, kc_a, vc_a, w_q, w_k, w_v, w_o, True)
        out_b = request(x_b, kc_b, vc_b, w_q, w_k, w_v, w_o, False)
        return out_a + out_b

    row_spec = P(("dp", "cp"), None)
    kv_spec = P(("dp", "cp"), None, None)
    full_spec = P()
    return jax.shard_map(local_step, mesh=mesh, in_specs=(row_spec, kv_spec, kv_spec, row_spec, kv_spec, kv_spec, full_spec, full_spec, full_spec, full_spec), out_specs=(row_spec, kv_spec, kv_spec, row_spec, kv_spec, kv_spec), check_vma=False)
```

profile of v0, /device:TPU:96, one launch (start us, length us, event | category | flops | bytes accessed | tf_op | source)
XLA Modules:
  0.0 1702.3 jit_solution(13106178573914609424)
XLA Ops:
  28.7 12.8 fusion.77
  47.7 429.5 %while.66 = (s32[]{:T(128)}, bf16[16,8,4,128]{3,0,2,1:T(8,128)(2,1)}, f32[16,8,4,128]{3,0,2,1:T(8,128)}, f32[16,8,4]{0,2,1:T(4,128)S(1)}, bf16[512,8,128]{2,0,1:...) while((s32[]{:T(128)}, bf16[16,8,4,128]{3,0,2,1:T(8,128)(2,1)}, f32[16,8,4,128]{3,0,2,1:T(8,128)}, ...), condition=%wide.region_11.12_spmd, body=%wide.region_8.11_spmd.sunk | while | flops 136058368 | bytes 7776453 | solution.py:93
  134.0 10.5 collective-permute-done
  155.9 10.5 collective-permute-done
  486.4 17.2 %fusion.76 = f32[256,4096]{1,0:T(8,128)} fusion(bf16[256,4096]{1,0:T(8,128)(2,1)S(1)} %copy-done, bf16[4096,4096]{1,0:T(8,128)(2,1)} %param.24), kind=kOutput, calls=%fused_computation.107 | convolution fusion | flops 8592031744 | bytes 39845888 | tf_op jit(solution)/shard_map/dot_general | solution.py:27
  528.6 650.0 %while.67 = (s32[]{:T(128)}, bf16[128,8,128]{2,0,1:T(8,128)(2,1)S(1)}, bf16[128,8,128]{2,0,1:T(8,128)(2,1)}, f32[256,8,4,128]{3,0,2,1:T(8,128)}, f32[256,8,4]{0,...) while((s32[]{:T(128)}, bf16[128,8,128]{2,0,1:T(8,128)(2,1)S(1)}, ...), condition=%wide.region_23.24_spmd, body=%wide.region_20.23_spmd.sunk | while | flops 549543936 | bytes 60850388 | solution.py:106
  529.0 14.6 collective-permute-done.3
  560.7 9.1 collective-permute-done.3
  601.9 9.1 collective-permute-done.3
  622.5 9.1 collective-permute-done.3
  663.7 9.1 collective-permute-done.3
  684.2 9.1 collective-permute-done.3
  704.8 9.1 collective-permute-done.3
  725.4 9.1 collective-permute-done.3
  766.6 9.1 collective-permute-done.3
  828.4 9.1 collective-permute-done.3
  869.6 9.1 collective-permute-done.3
  890.2 9.1 collective-permute-done.3
  910.8 9.1 collective-permute-done.3
  931.4 9.1 collective-permute-done.3
  972.6 9.1 collective-permute-done.3
  993.2 9.1 collective-permute-done.3
  1034.4 9.1 collective-permute-done.3
  1055.0 9.1 collective-permute-done.3
  1075.6 9.1 collective-permute-done.3
  1096.1 9.1 collective-permute-done.3
  1188.9 82.1 %while.68 = (s32[]{:T(128)}, f32[16,8,4,128]{3,0,2,1:T(8,128)S(1)}, f32[16,8,4]{0,2,1:T(4,128)S(1)}, bf16[32,16,8,128]{3,1,2,0:T(8,128)(2,1)}, bf16[16,8,4,128]{...) while((s32[]{:T(128)}, f32[16,8,4,128]{3,0,2,1:T(8,128)S(1)}, ...), condition=%wide.region_5.6_spmd.clone, body=%wide.region_2.5_spmd.clone.sunk | while | flops 4536102 | bytes 855467 | solution.py:75
  1272.4 13.5 convolution_convert_fusion.2
  1285.9 9.6 copy.87
  1306.0 22.7 %copy.86 = bf16[32,256,8,128]{1,3,2,0:T(8,128)(2,1)} copy(bf16[32,256,8,128]{3,2,1,0:T(8,128)(2,1)} %all-gather.9.cloned.1.call-done) | data formatting | bytes 33554432 | tf_op jit(solution)/shard_map/all_gather | solution.py:115
  1336.5 337.3 %while.69 = (s32[]{:T(128)}, f32[256,8,4,128]{0,3,2,1:T(8,128)}, f32[256,8,4]{0,2,1:T(4,128)S(1)}, bf16[32,256,8,128]{3,1,2,0:T(8,128)(2,1)}, bf16[256,8,4,128]{...) while((s32[]{:T(128)}, f32[256,8,4,128]{0,3,2,1:T(8,128)}, ...), condition=%wide.region_17.18_spmd.clone, body=%wide.region_14.17_spmd.clone.sunk | while | flops 1105355264 | bytes 71078112 | solution.py:75
  1678.4 16.9 convolution_convert_fusion
  (1492 shorter events, 1380.1 us)
Async XLA Ops:
  7.2 1176.7 %all-gather.7.cloned.1.call-start = ((), (), s32[]{:S(2)}) async-start(), calls=%async_computation.1 | async-start | bytes 1081344 | tf_op jit(solution)/shard_map/all_gather | solution.py:115
  13.7 1172.7 %all-gather.5.cloned.1.call-start = ((), (), s32[]{:S(2)}) async-start(), calls=%async_computation | async-start | bytes 1081344 | tf_op jit(solution)/shard_map/all_gather | solution.py:115
  19.1 1266.8 %all-gather.11.cloned.1.call-start = ((), (), s32[]{:S(2)}) async-start(), calls=%async_computation.3 | async-start | bytes 17301504 | tf_op jit(solution)/shard_map/all_gather | solution.py:115
  28.3 1277.7 %all-gather.9.cloned.1.call-start = ((), (), s32[]{:S(2)}) async-start(), calls=%async_computation.2 | async-start | bytes 17301504 | tf_op jit(solution)/shard_map/all_gather | solution.py:115
  102.0 16.3 collective-permute-start.1
  134.0 19.5 %collective-permute-start.1 = (f32[16,8,4,128]{3,0,2,1:T(8,128)}, f32[16,8,4,128]{3,0,2,1:T(8,128)}, u32[]{:S(2)}, u32[]{:S(2)}) collective-permute-start(f32[16,8,4,128]{3,0,2,1:T(8,128)} %get-tuple-element.917), channel_id=1, source_target_pairs={{0,1},{1,2},{2,3},{3,4},{4,5},{5,6},{6,7},{7,8},{8,9},{9,10},{10,1... | collective-permute-start | bytes 786440 | tf_op jit(solution)/shard_map/while/body/eval_jaxpr/ppermute | solution.py:87
  155.8 18.0 %collective-permute-start.1 = (f32[16,8,4,128]{3,0,2,1:T(8,128)}, f32[16,8,4,128]{3,0,2,1:T(8,128)}, u32[]{:S(2)}, u32[]{:S(2)}) collective-permute-start(f32[16,8,4,128]{3,0,2,1:T(8,128)} %get-tuple-element.917), channel_id=1, source_target_pairs={{0,1},{1,2},{2,3},{3,4},{4,5},{5,6},{6,7},{7,8},{8,9},{9,10},{10,1... | collective-permute-start | bytes 786440 | tf_op jit(solution)/shard_map/while/body/eval_jaxpr/ppermute | solution.py:87
  477.2 793.8 %collective-permute-start.5 = (f32[16,8,4]{0,2,1:T(4,128)S(1)}, f32[16,8,4]{0,2,1:T(4,128)S(1)}, u32[]{:S(2)}, u32[]{:S(2)}) collective-permute-start(f32[16,8,4]{0,2,1:T(4,128)S(1)} %get-tuple-element.472), channel_id=1, source_target_pairs={{0,1},{1,2},{2,3},{3,4},{4,5},{5,6},{6,7},{7,8},{8,9},{9,10},{10,1... | collective-permute-start | bytes 6152 | tf_op jit(solution)/shard_map/ppermute | solution.py:94
  477.2 793.9 %collective-permute-start.6 = (f32[16,8,4,128]{3,0,2,1:T(8,128)}, f32[16,8,4,128]{3,0,2,1:T(8,128)}, u32[]{:S(2)}, u32[]{:S(2)}) collective-permute-start(f32[16,8,4,128]{3,0,2,1:T(8,128)} %get-tuple-element.473), channel_id=1, source_target_pairs={{0,1},{1,2},{2,3},{3,4},{4,5},{5,6},{6,7},{7,8},{8,9},{9,10},{10,1... | collective-permute-start | bytes 786440 | tf_op jit(solution)/shard_map/ppermute | solution.py:94
  528.8 14.8 collective-permute-start.3
  528.9 23.1 %collective-permute-start.4 = (bf16[128,8,128]{2,0,1:T(8,128)(2,1)}, bf16[128,8,128]{2,0,1:T(8,128)(2,1)S(1)}, u32[]{:S(2)}, u32[]{:S(2)}) collective-permute-start(bf16[128,8,128]{2,0,1:T(8,128)(2,1)} %get-tuple-element.971), channel_id=1, source_target_pairs={{0,1},{1,2},{2,3},{3,4},{4,5},{5,6},{6,7},{7,8},{8,9},{9,10},{10,1... | collective-permute-start | bytes 786440 | tf_op jit(solution)/shard_map/while/body/eval_jaxpr/ppermute | solution.py:101
  560.7 11.9 collective-permute-start.4
  581.3 11.9 collective-permute-start.4
  601.9 11.9 collective-permute-start.4
  622.5 11.9 collective-permute-start.4
  643.1 11.9 collective-permute-start.4
  663.6 11.9 collective-permute-start.4
  704.8 11.9 collective-permute-start.4
  746.0 11.9 collective-permute-start.4
  766.6 11.9 collective-permute-start.4
  787.2 11.9 collective-permute-start.4
  807.8 11.9 collective-permute-start.4
  828.4 11.9 collective-permute-start.4
  849.0 11.9 collective-permute-start.4
  869.6 11.9 collective-permute-start.4
  910.8 11.9 collective-permute-start.4
  931.4 11.9 collective-permute-start.4
  952.0 11.9 collective-permute-start.4
  972.6 11.9 collective-permute-start.4
  993.2 11.9 collective-permute-start.4
  1013.8 11.9 collective-permute-start.4
  1034.4 11.9 collective-permute-start.4
  (274 other events, 1621.5 us)
Sparse Core Ops, SparseCore 0:
  13.9 39.9 all-gather.6
  56.5 38.1 all-gather.4
  96.8 78.4 all-gather.10
  484.7 74.7 all-gather.8
where the time goes:
time: 1720 us; the launch traced here: 1700 us
  matrix products  667 us (39%)
  waiting for transfers between devices  607 us (35%)
  local copies, waits for them, and re-layouts  237 us (14%)
  other arithmetic  167 us (10%)
    dot_general x128, matrix products, block_attend(): jnp.einsum('tkgs,skd->tkgd', exp_s.astype(jnp.bfloat16), blk_vals, prefer...  431 us
    ppermute x31, waiting for transfers between devices, visit(): blk_keys = lax.ppermute(loop_carry[0], 'cp', next_perm)  288 us
    ppermute x31, waiting for transfers between devices, visit(): q_cur = lax.ppermute(loop_carry[0], 'cp', next_perm)  244 us
    while x341, local copies, waits for them, and re-layouts  167 us
    dot_general x128, matrix products, block_attend(): jnp.einsum('tkgd,skd->tkgs', q_grp, blk_keys, preferred_element_type=jnp....  155 us
    reduce_sum x128, other arithmetic, block_attend(): row_sum = jnp.sum(exp_s, axis=-1)  110 us
    ppermute x31, waiting for transfers between devices, visit(): blk_vals = lax.ppermute(loop_carry[1], 'cp', next_perm)  39.6 us
    ppermute x31, waiting for transfers between devices, visit(): acc_o = lax.ppermute(loop_carry[1], 'cp', next_perm)  35.2 us
  transfers between devices with their start and end apart: 161, of which 124 were waited for; matrix products, arithmetic and copies ran while one was open for 36% of the time, Pallas kernels for 0%

commit v1 on v0

v1 whole, which is shorter than its diff:
```python
import functools

import jax
import jax.numpy as jnp
from jax import lax
from jax.experimental import pallas as pl
from jax.experimental.pallas import tpu as pltpu
from jax.sharding import PartitionSpec as P

ROPE_BASE = 500000
LOG2E = 1.4426950408889634
NEG = float(jnp.finfo(jnp.float32).min)
MESH = pl.DeviceIdType.MESH
CORES = 2
VMEM_LIMIT = 62 * 1024 * 1024


def rope_tables(positions, head_dim):
    half_dim = head_dim // 2
    inv_freq = jnp.power(jnp.float32(ROPE_BASE), jnp.arange(half_dim, dtype=jnp.float32) * (-2.0 / head_dim))
    angles = positions.astype(jnp.float32)[:, None] * inv_freq[None, :]
    return jnp.cos(angles), jnp.sin(angles)


def rotary(lin, cos_ang, sin_ang, head_dim):
    n_tok = lin.shape[0]
    half_dim = head_dim // 2
    x = lin.reshape(n_tok, -1, head_dim).astype(jnp.float32)
    a, b = x[..., :half_dim], x[..., half_dim:]
    c, s = cos_ang[:, None, :], sin_ang[:, None, :]
    out = jnp.concatenate([a * c - b * s, b * c + a * s], axis=-1)
    return out.astype(jnp.bfloat16).reshape(n_tok, -1)


def qk(keys, queries):
    return lax.dot_general(keys, queries, (((1,), (1,)), ((), ())), preferred_element_type=jnp.float32)


def soft_step(scale2, s, vt, m, l, acc_ref):
    m_new = jnp.maximum(m, jnp.max(s, axis=0, keepdims=True))
    alpha = jnp.exp2((m - m_new) * scale2)
    e = jnp.exp2((s - m_new) * scale2)
    l_new = l * alpha + jnp.sum(e, axis=0, keepdims=True)
    pv = jnp.dot(vt, e.astype(jnp.bfloat16), preferred_element_type=jnp.float32)
    acc_ref[...] = acc_ref[...] * alpha + pv
    return m_new, l_new


def kernel(dims, qb, kb, vb, kcb, vcb, qa, ka, va, kca, vca, ob, oa,
           qbuf, kc, vc, kn, vn, vtc, vtn, obuf, acc, m_all, l_all, q_s, s0, s1,
           qabuf, kac, vac, kan, van, vtac, vtan, oastage, ststage, oarecv, strecv,
           send_sem, recv_sem):
    ny, nx, kv, grp, dim = dims
    cp = ny * nx * CORES
    tb = qb.shape[0]
    tq = tb // 2
    rows = grp * tq
    width = grp * dim
    cb = kcb.shape[0]
    ta = qa.shape[0]
    ca = kca.shape[0]
    scale2 = dim ** -0.5 * LOG2E

    me = lax.axis_index("cp")
    c = lax.rem(me, CORES)
    x = lax.rem(me // CORES, nx)
    y = me // (CORES * nx)
    hb = y * CORES + c
    ha = x * CORES + c

    def dev(yy, xx, cc):
        return (yy * nx + xx) * CORES + cc

    def peer_y(h):
        return dev(h // CORES, x, lax.rem(h, CORES))

    def peer_x(h):
        return dev(y, h // CORES, lax.rem(h, CORES))

    def put(item, src, dst, target):
        pltpu.make_async_remote_copy(
            src_ref=src, dst_ref=dst, send_sem=send_sem.at[item], recv_sem=recv_sem.at[item],
            device_id={"cp": target}, device_id_type=MESH,
        ).start()

    def local(item, src, dst):
        pltpu.make_async_copy(src, dst, recv_sem.at[item]).start()

    def wait_in(item, ref):
        pltpu.make_async_copy(ref, ref, recv_sem.at[item]).wait()

    def wait_out(item, ref):
        pltpu.make_async_copy(ref, ref, send_sem.at[item]).wait()

    KC, VC, Q, KN, VN, KAC, VAC, KAN, VAN, QA, OB, OA, ST = range(13)
    AG = 13

    barrier = pltpu.get_barrier_semaphore()

    def greet(d, _):
        pl.semaphore_signal(barrier, inc=1, device_id={"cp": d}, device_id_type=MESH)
        return 0

    lax.fori_loop(0, cp, greet, 0)
    pl.semaphore_wait(barrier, cp)

    def head_cols(ref, h, w):
        return ref.at[:, pl.ds(pl.multiple_of(h * w, w), w)]

    def scatter(item, src, w, dst, mine, peer):
        def one(k, _):
            h = lax.rem(mine + k, kv)
            put(item, head_cols(src, h, w), dst, peer(h))
            return 0

        lax.fori_loop(1, kv, one, 0)
        local(item, head_cols(src, mine, w), dst)

    def scatter_qa(k, _):
        d = lax.rem(me + k, cp)
        h = lax.rem(d, CORES * nx)
        put(QA, head_cols(qa, h, width), qabuf.at[pl.ds(pl.multiple_of(me * ta, ta), ta), :], d)
        return 0

    lax.fori_loop(1, cp, scatter_qa, 0)
    local(QA, head_cols(qa, ha, width), qabuf.at[pl.ds(pl.multiple_of(me * ta, ta), ta), :])
    a_rows = pl.ds(pl.multiple_of(ha * ta, ta), ta)
    scatter(KC, kcb, dim, kc.at[y, x, pl.ds(pl.multiple_of(c * cb, cb), cb), :], hb, peer_y)
    scatter(VC, vcb, dim, vc.at[y, x, pl.ds(pl.multiple_of(c * cb, cb), cb), :], hb, peer_y)
    scatter(KAN, ka, dim, kan.at[a_rows, :], ha, peer_x)
    scatter(VAN, va, dim, van.at[a_rows, :], ha, peer_x)
    scatter(KAC, kca, dim, kac.at[ha], ha, peer_x)
    scatter(VAC, vca, dim, vac.at[ha], ha, peer_x)
    scatter(Q, qb, width, qbuf.at[hb], hb, peer_y)
    scatter(KN, kb, dim, kn.at[y, x, pl.ds(pl.multiple_of(c * tb, tb), tb), :], hb, peer_y)
    scatter(VN, vb, dim, vn.at[y, x, pl.ds(pl.multiple_of(c * tb, tb), tb), :], hb, peer_y)

    right = dev(y, lax.rem(x + 1, nx), c)
    left = dev(y, lax.rem(x + nx - 1, nx), c)
    x_left = lax.rem(x + nx - 1, nx)
    x_right = lax.rem(x + 1, nx)
    x_far = lax.rem(x + nx // 2, nx)
    lo, hi = pl.ds(0, ny // 2), pl.ds(ny // 2, ny // 2)

    def ag_sem(i, step, direction):
        return AG + i * 4 + step * 2 + direction

    def ring_first(i, buf):
        put(ag_sem(i, 0, 0), buf.at[:, x], buf.at[:, x], right)
        put(ag_sem(i, 0, 1), buf.at[:, x], buf.at[:, x], left)

    def ring_second(i, buf):
        wait_in(ag_sem(i, 0, 0), buf.at[:, x_left])
        put(ag_sem(i, 1, 0), buf.at[lo, x_left], buf.at[lo, x_left], right)
        wait_in(ag_sem(i, 0, 1), buf.at[:, x_right])
        put(ag_sem(i, 1, 1), buf.at[hi, x_right], buf.at[hi, x_right], left)

    def ring_last(i, buf):
        wait_in(ag_sem(i, 1, 0), buf.at[lo, x_far])
        wait_in(ag_sem(i, 1, 1), buf.at[hi, x_far])

    def ring_drain(i, buf):
        wait_out(ag_sem(i, 0, 0), buf.at[:, x])
        wait_out(ag_sem(i, 0, 1), buf.at[:, x])
        wait_out(ag_sem(i, 1, 0), buf.at[lo, x])
        wait_out(ag_sem(i, 1, 1), buf.at[hi, x])

    wait_in(KC, kc.at[:, x])
    ring_first(0, kc)
    wait_in(VC, vc.at[:, x])
    ring_first(1, vc)

    def load_q(src, t0):
        for half in range(2):
            for g in range(grp):
                q_s[half, pl.ds(g * tq, tq), :] = src[pl.ds(t0 + half * tq, tq), pl.ds(g * dim, dim)]

    def two_tiles(n, k_at, v_at, acc0, acc1, state, masks):
        s0[...] = qk(k_at(0), q_s[0])

        def body(j, carry):
            m0, l0, m1, l1 = carry
            s1[...] = qk(k_at(j), q_s[1])
            m0, l0 = soft_step(scale2, s0[...], v_at(j), m0, l0, acc0)
            s0[...] = qk(k_at(j + 1), q_s[0])
            m1, l1 = soft_step(scale2, s1[...], v_at(j), m1, l1, acc1)
            return m0, l0, m1, l1

        m0, l0, m1, l1 = lax.fori_loop(0, n - 1, body, state)
        s1[...] = qk(k_at(n - 1), q_s[1])
        e0, e1 = s0[...], s1[...]
        if masks is not None:
            e0 = jnp.where(masks[0], e0, NEG)
            e1 = jnp.where(masks[1], e1, NEG)
        m0, l0 = soft_step(scale2, e0, v_at(n - 1), m0, l0, acc0)
        m1, l1 = soft_step(scale2, e1, v_at(n - 1), m1, l1, acc1)
        return m0, l0, m1, l1

    def fresh(acc0, acc1):
        acc0[...] = jnp.zeros_like(acc0)
        acc1[...] = jnp.zeros_like(acc1)
        neg = jnp.full((1, rows), NEG, jnp.float32)
        zero = jnp.zeros((1, rows), jnp.float32)
        return neg, zero, neg, zero

    def token_of_lane(shape):
        return lax.rem(lax.broadcasted_iota(jnp.int32, shape, 1), tq)

    wait_in(QA, qabuf)
    wait_in(KAC, kac)
    wait_in(VAC, vac)
    wait_in(KAN, kan)
    wait_in(VAN, van)

    def turn_a(j, _):
        vtac[j] = vac[j].T
        return 0

    lax.fori_loop(0, kv, turn_a, 0)
    vtan[...] = van[...].T
    new_a = kan.shape[0]

    def unit_a(u, _):
        t0 = pl.multiple_of(u * 2 * tq, 2 * tq)
        load_q(qabuf, t0)
        acc0, acc1 = acc.at[0], acc.at[1]
        state = fresh(acc0, acc1)
        m0, l0, m1, l1 = two_tiles(kv, lambda j: kac[j], lambda j: vtac[j], acc0, acc1, state, None)
        pos_k = y * new_a + lax.broadcasted_iota(jnp.int32, (new_a, rows), 0)
        pos_q = t0 + token_of_lane((new_a, rows))
        out = []
        for half, (m, l, a_ref) in enumerate(((m0, l0, acc0), (m1, l1, acc1))):
            s = jnp.where(pos_k <= pos_q + half * tq, qk(kan[...], q_s[half]), NEG)
            m, l = soft_step(scale2, s, vtan[...], m, l, a_ref)
            out.append((m, l))
        for half, (m, l) in enumerate(out):
            r = pl.ds(pl.multiple_of(t0 + half * tq, tq), tq)
            row = lax.broadcasted_iota(jnp.int32, (dim, tq), 0)
            stat = jnp.zeros((dim, tq), jnp.float32)
            for g in range(grp):
                cols = slice(g * tq, (g + 1) * tq)
                oastage[r, pl.ds(g * dim, dim)] = acc[half, :, pl.ds(g * tq, tq)].T
                stat = jnp.where(row == g, m[:, cols], stat)
                stat = jnp.where(row == grp + g, l[:, cols], stat)
            ststage[r, :] = stat.T
        return 0

    lax.fori_loop(0, cp * ta // (2 * tq), unit_a, 0)

    slot = y * kv + ha

    def give_a(k, _):
        d = lax.rem(me + k, cp)
        r = pl.ds(pl.multiple_of(d * ta, ta), ta)
        put(OA, oastage.at[r, :], oarecv.at[slot], d)
        put(ST, ststage.at[r, :], strecv.at[slot], d)
        return 0

    lax.fori_loop(1, cp, give_a, 0)
    r_me = pl.ds(pl.multiple_of(me * ta, ta), ta)
    local(OA, oastage.at[r_me, :], oarecv.at[slot])
    local(ST, ststage.at[r_me, :], strecv.at[slot])

    ring_second(0, kc)
    ring_second(1, vc)
    wait_in(KN, kn.at[:, x])
    ring_first(2, kn)
    wait_in(VN, vn.at[:, x])
    ring_first(3, vn)
    wait_in(Q, qbuf)
    ring_last(0, kc)
    ring_last(1, vc)

    blocks = vtc.shape[0]
    per_row = blocks // ny
    per_blk = nx // per_row
    blk = per_blk * CORES * cb

    def cached(buf, j):
        return buf[j // per_row, pl.ds(lax.rem(j, per_row) * per_blk, per_blk)].reshape(blk, dim)

    def turn_c(j, _):
        vtc[j] = cached(vc, j).T
        return 0

    lax.fori_loop(0, blocks, turn_c, 0)

    def keep(u, state):
        for half in range(2):
            m_all[2 * u + half, 0:1, :] = state[2 * half]
            l_all[2 * u + half, 0:1, :] = state[2 * half + 1]

    def unit_c(u, _):
        load_q(qbuf.at[u], 0)
        acc0, acc1 = acc.at[2 * u], acc.at[2 * u + 1]
        state = fresh(acc0, acc1)
        keep(u, two_tiles(blocks, lambda j: cached(kc, j), lambda j: vtc[j], acc0, acc1, state, None))
        return 0

    lax.fori_loop(0, kv // 2, unit_c, 0)
    ring_second(2, kn)
    ring_second(3, vn)
    lax.fori_loop(kv // 2, kv, unit_c, 0)
    ring_last(2, kn)
    ring_last(3, vn)

    def turn_n(j, _):
        vtn[j] = vn[j // nx, lax.rem(j, nx)].T
        return 0

    lax.fori_loop(0, ny * nx, turn_n, 0)
    blk_n = CORES * tb

    def unit_n(i, _):
        u = lax.rem(hb + 1 + i, kv)
        yy, cc = u // CORES, lax.rem(u, CORES)
        last = yy * nx + x
        load_q(qbuf.at[u], 0)
        acc0, acc1 = acc.at[2 * u], acc.at[2 * u + 1]
        state = (m_all[2 * u, 0:1, :], l_all[2 * u, 0:1, :], m_all[2 * u + 1, 0:1, :], l_all[2 * u + 1, 0:1, :])
        pos_k = lax.broadcasted_iota(jnp.int32, (blk_n, rows), 0)
        pos_q = cc * tb + token_of_lane((blk_n, rows))
        masks = (pos_k <= pos_q, pos_k <= pos_q + tq)
        m0, l0, m1, l1 = two_tiles(
            last + 1, lambda j: kn[j // nx, lax.rem(j, nx)], lambda j: vtn[j], acc0, acc1, state, masks)
        for half, l in enumerate((l0, l1)):
            inv = 1.0 / l
            for g in range(grp):
                cols = pl.ds(g * tq, tq)
                o = acc[2 * u + half, :, cols] * inv[:, g * tq:(g + 1) * tq]
                obuf[u, pl.ds(half * tq, tq), pl.ds(g * dim, dim)] = o.T.astype(obuf.dtype)

        @pl.when(i < kv - 1)
        def _():
            put(OB, obuf.at[u], head_cols(ob, hb, width), peer_y(u))

        @pl.when(i == kv - 1)
        def _():
            local(OB, obuf.at[u], head_cols(ob, hb, width))

        return 0

    lax.fori_loop(0, kv, unit_n, 0)

    wait_in(OA, oarecv)
    wait_in(ST, strecv)

    def merge_a(h, _):
        for g in range(grp):
            ms = [strecv[i * kv + h, :, g:g + 1] for i in range(ny)]
            ls = [strecv[i * kv + h, :, grp + g:grp + g + 1] for i in range(ny)]
            top = functools.reduce(jnp.maximum, ms)
            num = jnp.zeros((ta, dim), jnp.float32)
            den = jnp.zeros((ta, 1), jnp.float32)
            for i in range(ny):
                w = jnp.exp2((ms[i] - top) * scale2)
                num = num + w * oarecv[i * kv + h, :, pl.ds(g * dim, dim)]
                den = den + w * ls[i]
            oa[:, pl.ds(pl.multiple_of(h * width + g * dim, dim), dim)] = (num / den).astype(oa.dtype)
        return 0

    lax.fori_loop(0, kv, merge_a, 0)

    wait_in(OB, ob)
    most = kv - 1
    wait_out(KC, kcb.at[:, pl.ds(0, most * dim)])
    wait_out(VC, vcb.at[:, pl.ds(0, most * dim)])
    wait_out(KN, kb.at[:, pl.ds(0, most * dim)])
    wait_out(VN, vb.at[:, pl.ds(0, most * dim)])
    wait_out(Q, qb.at[:, pl.ds(0, most * width)])
    wait_out(KAC, kca.at[:, pl.ds(0, most * dim)])
    wait_out(VAC, vca.at[:, pl.ds(0, most * dim)])
    wait_out(KAN, ka.at[:, pl.ds(0, most * dim)])
    wait_out(VAN, va.at[:, pl.ds(0, most * dim)])
    wait_out(QA, qabuf.at[pl.ds(0, (cp - 1) * ta), :])
    wait_out(OB, obuf.at[pl.ds(0, most)])
    wait_out(OA, oarecv.at[pl.ds(0, cp - 1)])
    wait_out(ST, strecv.at[pl.ds(0, cp - 1)])
    ring_drain(0, kc)
    ring_drain(1, vc)
    ring_drain(2, kn)
    ring_drain(3, vn)


def attention(cp, kv, dim, qb, kb, vb, kcb, vcb, qa, ka, va, kca, vca):
    ny, nx = kv // CORES, cp // kv
    assert nx * CORES == kv and ny * nx * CORES == cp
    grp = qb.shape[1] // (kv * dim)
    tb, ta, cb, ca = qb.shape[0], qa.shape[0], kcb.shape[0], kca.shape[0]
    tq = tb // 2
    rows, width = grp * tq, grp * dim
    blk = CORES * tb
    assert blk == ca and (ny * nx * CORES * cb) % (ny * blk) == 0 and (cp * ta) % (2 * tq) == 0
    bf, f32 = jnp.bfloat16, jnp.float32
    vm = pltpu.VMEM
    scratch = [
        vm((kv, tb, width), bf),
        vm((ny, nx, CORES * cb, dim), bf),
        vm((ny, nx, CORES * cb, dim), bf),
        vm((ny, nx, blk, dim), bf),
        vm((ny, nx, blk, dim), bf),
        vm((cp * cb // blk, dim, blk), bf),
        vm((ny * nx, dim, blk), bf),
        vm((kv, tb, width), bf),
        vm((2 * kv, dim, rows), f32),
        vm((2 * kv, 8, rows), f32),
        vm((2 * kv, 8, rows), f32),
        vm((2, rows, dim), bf),
        vm((blk, rows), f32),
        vm((blk, rows), f32),
        vm((cp * ta, width), bf),
        vm((kv, ca, dim), bf),
        vm((kv, ca, dim), bf),
        vm((kv * ta, dim), bf),
        vm((kv * ta, dim), bf),
        vm((kv, dim, ca), bf),
        vm((dim, kv * ta), bf),
        vm((cp * ta, width), f32),
        vm((cp * ta, dim), f32),
        vm((cp, ta, width), f32),
        vm((cp, ta, dim), f32),
        pltpu.SemaphoreType.DMA((29,)),
        pltpu.SemaphoreType.DMA((29,)),
    ]
    any_spec = pl.BlockSpec(memory_space=pl.ANY)
    return pl.pallas_call(
        functools.partial(kernel, (ny, nx, kv, grp, dim)),
        out_shape=(jax.ShapeDtypeStruct(qb.shape, bf), jax.ShapeDtypeStruct(qa.shape, bf)),
        in_specs=[any_spec] * 10,
        out_specs=(any_spec, pl.BlockSpec(memory_space=pltpu.VMEM)),
        scratch_shapes=scratch,
        compiler_params=pltpu.CompilerParams(
            collective_id=0, has_side_effects=True, vmem_limit_bytes=VMEM_LIMIT),
        name="attend",
    )(qb, kb, vb, kcb, vcb, qa, ka, va, kca, vca)


def solution(mesh):
    cp_size = mesh.shape["cp"]

    def local_step(x_a, kc_a, vc_a, x_b, kc_b, vc_b, w_q, w_k, w_v, w_o):
        ta, tb = x_a.shape[0], x_b.shape[0]
        kv, dim = kc_a.shape[1:]
        me = lax.axis_index("cp")
        pos_a = kc_a.shape[0] * cp_size + me * ta + jnp.arange(ta)
        pos_b = kc_b.shape[0] * cp_size + me * tb + jnp.arange(tb)
        cos_ang, sin_ang = rope_tables(jnp.concatenate([pos_b, pos_a]), dim)
        x = jnp.concatenate([x_b, x_a], axis=0)

        def proj(w):
            return jnp.dot(x, w, preferred_element_type=jnp.float32).astype(jnp.bfloat16)

        q = rotary(proj(w_q), cos_ang, sin_ang, dim)
        k = rotary(proj(w_k), cos_ang, sin_ang, dim)
        v = proj(w_v)
        flat = lambda t: t.reshape(t.shape[0], kv * dim)
        o_b, o_a = attention(
            cp_size, kv, dim, q[:tb], k[:tb], v[:tb], flat(kc_b), flat(vc_b),
            q[tb:], k[tb:], v[tb:], flat(kc_a), flat(vc_a))
        o = jnp.concatenate([o_b, o_a], axis=0)
        y = jnp.dot(o, w_o, preferred_element_type=jnp.float32).astype(jnp.bfloat16)
        heads = lambda t: t.reshape(t.shape[0], kv, dim)
        return y[tb:], heads(k[tb:]), heads(v[tb:]), y[:tb], heads(k[:tb]), heads(v[:tb])

    row_spec = P(("dp", "cp"), None)
    kv_spec = P(("dp", "cp"), None, None)
    full_spec = P()
    return jax.shard_map(
        local_step, mesh=mesh,
        in_specs=(row_spec, kv_spec, kv_spec, row_spec, kv_spec, kv_spec, full_spec, full_spec, full_spec, full_spec),
        out_specs=(row_spec, kv_spec, kv_spec, row_spec, kv_spec, kv_spec), check_vma=False)
```

time: 1720 us -> 266 us (0.15)
  the two profiles are of different devices: /device:TPU:96 before, /device:TPU:103 now
where the time goes in v1:
time: 266 us; the launch traced here: 265 us
  Pallas kernels  197 us (74%)
  matrix products  40.6 us (15%)
  local copies, waits for them, and re-layouts  18.2 us (7%)
  other arithmetic  8.21 us (3%)
    pallas_call x1, Pallas kernels, attention(): pl.pallas_call(functools.partial(kernel, (ny, nx, kv, grp, dim)), out_sha...  197 us
    dot_general x3, matrix products, proj(): jnp.dot(x, w, preferred_element_type=jnp.float32).astype(jnp.bfloat16)  24.6 us
    dot_general x1, matrix products, local_step(): y = jnp.dot(o, w_o, preferred_element_type=jnp.float32).astype(jnp.bfloat16)  16 us
    unnamed x33, local copies, waits for them, and re-layouts  13.4 us
    another operation x2, other arithmetic  5.98 us

profile of v1, /device:TPU:103, one launch (start us, length us, event | category | flops | bytes accessed | tf_op | source)
XLA Modules:
  0.0 265.1 jit_solution(7037309978974728954)
XLA Ops:
  0.6 0.0 copy-start.8
  0.6 1.8 constant_dynamic-update-slice_fusion.1
  2.4 16.1 %fusion.4 = f32[34,8,32,128]{3,1,2,0:T(8,128)S(1)} fusion(bf16[272,4096]{1,0:T(8,128)(2,1)S(1)} %constant_dynamic-update-slice_fusion, bf16[4096,4096]{1,0:T(8,128)(2,1)} %param.16), kind=kOutput, calls=%fused_computation.10 | convolution fusion | flops 9129033728 | bytes 40239104 | tf_op jit(solution)/shard_map/dot_general | solution.py:451
  18.6 2.8 %copy.16 = f32[34,8,32,128]{3,2,1,0:T(8,128)} copy(f32[34,8,32,128]{3,1,2,0:T(8,128)S(1)} %fusion.4) | data formatting | bytes 8912896
  21.5 0.6 multiply_cosine_fusion
  22.0 5.5 %add_convert_fusion = (bf16[272,32,64]{2,1,0:T(8,128)(2,1)S(1)}, bf16[272,32,64]{2,1,0:T(8,128)(2,1)S(1)}) fusion(f32[272,32,128]{2,1,0:T(8,128)} %bitcast.47, f32[272,64]{1,0:T(8,128)S(1)} %get-tuple-element.19, f32[272,64]{1,0:T(8,128)S(1)} %get-tuple-element.18), kind=kLoop, calls=%fused_computation.3 | loop fusion | flops 4456448 | bytes 6823936 | tf_op jit(solution)/shard_map/convert.5
  27.5 1.2 fusion.5
  28.7 0.0 slice-start
  28.7 2.3 copy.36
  31.0 6.0 %fusion.7 = f32[34,8,8,128]{3,1,2,0:T(8,128)S(1)} fusion(bf16[272,4096]{1,0:T(8,128)(2,1)S(1)} %constant_dynamic-update-slice_fusion, bf16[4096,1024]{1,0:T(8,128)(2,1)} %param.17), kind=kOutput, calls=%fused_computation.16 | convolution fusion | flops 2282258432 | bytes 11730944 | tf_op jit(solution)/shard_map/dot_general | solution.py:451
  37.0 0.2 copy.18
  37.2 0.5 add_convert_fusion.1
  37.8 0.3 fusion.8
  38.1 0.0 copy-start
  38.1 0.9 copy.37
  39.0 0.8 copy-done.2
  39.8 2.5 convolution_convert_fusion.2
  42.2 1.0 slice_bitcast_fusion.1
  43.3 0.9 copy_bitcast_fusion.4
  44.1 0.1 pad_maximum_fusion
  44.3 0.7 copy.38
  45.0 0.1 pad_maximum_fusion.1
  45.0 0.0 copy-start.7
  45.1 0.6 copy.39
  45.7 0.6 slice_bitcast_fusion
  46.3 1.8 copy_bitcast_fusion.1
  48.1 197.3 %attend.1 = (bf16[256,4096]{1,0:T(8,128)(2,1)}, bf16[16,4096]{1,0:T(8,128)(2,1)}) custom-call(bf16[256,4096]{1,0:T(8,128)(2,1)} %bitcast.49, bf16[256,1024]{1,0:T(8,128)(2,1)} %bitcast.52, bf16[256,1024]{1,0:T(8,128)(2,1)} %get-tuple-element.15.vb, bf16[128,1024]{1,0:T(8,128)(2,1)} %get-tuple-element.23.kcb, bf16[128,1024]{1,0:T(8,128)(2,1)} %get-tuple-element.22.vcb, ...), custom_call_target="tpu_custom_call" | custom-call | tf_op jit(solution)/shard_map/attend/pallas_call | solution.py:426
  245.5 16.0 %convolution_convert_fusion = bf16[272,4096]{1,0:T(8,128)(2,1)S(1)} fusion(bf16[4096,4096]{1,0:T(8,128)(2,1)} %param.19, bf16[16,4096]{1,0:T(8,128)(2,1)} %get-tuple-element.9, bf16[256,4096]{1,0:T(8,128)(2,1)} %get-tuple-element.8), kind=kOutput, calls=%fused_computation | convolution fusion | flops 9132376064 | bytes 38010880 | tf_op jit(solution)/shard_map/dot_general | solution.py:461
  261.5 0.7 slice.78
  262.2 0.6 copy.26
  262.8 1.5 slice.79
  264.2 0.9 copy.27
  (23 shorter events, 0.1 us)
Async XLA Ops:
  0.6 1.8 copy-start.8
  2.4 28.6 %copy-start.1 = (bf16[272,4096]{1,0:T(8,128)(2,1)}, bf16[272,4096]{1,0:T(8,128)(2,1)S(1)}, u32[]{:S(2)}) copy-start(bf16[272,4096]{1,0:T(8,128)(2,1)S(1)} %constant_dynamic-update-slice_fusion) | copy-start | bytes 6684676
  28.7 10.3 %slice-start = ((s8[8388608]{0:T(1024)(128)(4,1)}), s8[4194304]{0:T(1024)(128)(4,1)S(1)}, s32[]{:S(2)}) async-start(s8[8388608]{0:T(1024)(128)(4,1)} %bitcast.63), calls=%async_computation | async-start | bytes 8388608
  31.0 8.0 %slice-start.1 = ((s8[8388608]{0:T(1024)(128)(4,1)}), s8[4194304]{0:T(1024)(128)(4,1)S(1)}, s32[]{:S(2)}) async-start(s8[8388608]{0:T(1024)(128)(4,1)} %bitcast.63), calls=%async_computation.1 | async-start | bytes 8388608
  37.7 2.0 copy-start.2
  38.1 4.2 %copy-start = (bf16[256,8,128]{2,1,0:T(8,128)(2,1)}, bf16[256,8,128]{2,1,0:T(8,128)(2,1)S(1)}, u32[]{:S(2)}) copy-start(bf16[256,8,128]{2,1,0:T(8,128)(2,1)S(1)} %fusion.8) | copy-start | bytes 1572868
  39.8 3.5 %copy-start.5 = (bf16[128,8,128]{2,1,0:T(8,128)(2,1)S(1)}, bf16[128,8,128]{2,1,0:T(8,128)(2,1)}, u32[]{:S(2)}) copy-start(bf16[128,8,128]{2,1,0:T(8,128)(2,1)} %param.15) | copy-start | bytes 786436
  39.8 3.5 %copy-start.6 = (bf16[128,8,128]{2,1,0:T(8,128)(2,1)S(1)}, bf16[128,8,128]{2,1,0:T(8,128)(2,1)}, u32[]{:S(2)}) copy-start(bf16[128,8,128]{2,1,0:T(8,128)(2,1)} %param.14) | copy-start | bytes 786436
  44.1 2.2 copy-start.3
  44.1 2.2 copy-start.4
  45.0 200.4 %copy-start.7 = (bf16[16,8,128]{2,1,0:T(8,128)(2,1)}, bf16[16,8,128]{2,1,0:T(8,128)(2,1)S(1)}, u32[]{:S(2)}) copy-start(bf16[16,8,128]{2,1,0:T(8,128)(2,1)S(1)} %pad_maximum_fusion.1) | copy-start | bytes 98308

commit v2 on v1

v2 whole, which is shorter than its diff:
```python
import functools

import jax
import jax.numpy as jnp
from jax import lax
from jax.experimental import pallas as pl
from jax.experimental.pallas import tpu as pltpu
from jax.sharding import PartitionSpec as P

ROPE_BASE = 500000
LOG2E = 1.4426950408889634
NEG = float(jnp.finfo(jnp.float32).min)
MESH = pl.DeviceIdType.MESH
CORES = 2
VMEM_LIMIT = 62 * 1024 * 1024


def rope_tables(positions, head_dim):
    half_dim = head_dim // 2
    inv_freq = jnp.power(jnp.float32(ROPE_BASE), jnp.arange(half_dim, dtype=jnp.float32) * (-2.0 / head_dim))
    angles = positions.astype(jnp.float32)[:, None] * inv_freq[None, :]
    cos_ang, sin_ang = jnp.cos(angles), jnp.sin(angles)
    return jnp.concatenate([cos_ang, cos_ang], axis=1), jnp.concatenate([-sin_ang, sin_ang], axis=1)


def qk(keys, queries):
    return lax.dot_general(keys, queries, (((1,), (1,)), ((), ())), preferred_element_type=jnp.float32)


def fold(s, op):
    return functools.reduce(op, [s[i:i + 8] for i in range(0, s.shape[0], 8)])


def soft_step(scale2, s, vt, m, l, acc_ref):
    m_new = jnp.maximum(m, jnp.max(s, axis=0, keepdims=True))
    alpha = jnp.exp2((m - m_new) * scale2)
    e = jnp.exp2((s - m_new) * scale2)
    l_new = l * alpha + jnp.sum(e, axis=0, keepdims=True)
    pv = jnp.dot(vt, e.astype(jnp.bfloat16), preferred_element_type=jnp.float32)
    acc_ref[...] = acc_ref[...] * alpha + pv
    return m_new, l_new


def kernel(dims, xb, xa, cosf, sinf, wq, wk, wv, kcb, vcb, kca, vca, ob, oa, nkb, nvb, nka, nva,
           xs, wbuf, qsend, kvsend, rkb, rvb, rka, rva, tkb, tvb, tka, tva,
           qbuf, kc, vc, kn, vn, vtc, vtn, obuf, acc, m_all, l_all, q_s, s0, s1, p0, p1,
           qabuf, kac, vac, kan, van, vtac, vtan, oastage, ststage, oarecv, strecv,
           send_sem, recv_sem, load_sem, wsem, out_sem):
    ny, nx, kv, grp, dim = dims
    cp = ny * nx * CORES
    tb, ta = xb.shape[0], xa.shape[0]
    tq = tb // 2
    rows = grp * tq
    width = grp * dim
    pair = CORES * dim
    cb = kcb.shape[0]
    scale2 = dim ** -0.5 * LOG2E
    bf = jnp.bfloat16

    me = lax.axis_index("cp")
    c = lax.rem(me, CORES)
    x = lax.rem(me // CORES, nx)
    y = me // (CORES * nx)
    hb = y * CORES + c
    ha = x * CORES + c

    def dev(yy, xx, cc):
        return (yy * nx + xx) * CORES + cc

    def peer_y(h):
        return dev(h // CORES, x, lax.rem(h, CORES))

    def peer_x(h):
        return dev(y, h // CORES, lax.rem(h, CORES))

    def put(item, src, dst, target):
        pltpu.make_async_remote_copy(
            src_ref=src, dst_ref=dst, send_sem=send_sem.at[item], recv_sem=recv_sem.at[item],
            device_id={"cp": target}, device_id_type=MESH,
        ).start()

    def copy(src, dst, sem):
        pltpu.make_async_copy(src, dst, sem).start()

    def wait(ref, sem):
        pltpu.make_async_copy(ref, ref, sem).wait()

    def give(item, src, dst, target):
        @pl.when(target == me)
        def _():
            copy(src, dst, recv_sem.at[item])

        @pl.when(target != me)
        def _():
            put(item, src, dst, target)

    def wait_in(item, ref):
        wait(ref, recv_sem.at[item])

    def wait_out(item, ref):
        wait(ref, send_sem.at[item])

    KC, VC, Q, KN, VN, KAC, VAC, KAN, VAN, QA, OB, OA, ST = range(13)
    AG = 13

    barrier = pltpu.get_barrier_semaphore()

    def greet(d, _):
        pl.semaphore_signal(barrier, inc=1, device_id={"cp": d}, device_id_type=MESH)
        return 0

    raw = ((kcb, rkb, tkb), (vcb, rvb, tvb), (kca, rka, tka), (vca, rva, tva))
    for i, (src, dst, _) in enumerate(raw):
        copy(src, dst, load_sem.at[i])
    copy(xb, xs.at[pl.ds(0, tb), :], load_sem.at[4])
    copy(xa, xs.at[pl.ds(tb, ta), :], load_sem.at[4])

    q_steps, kv_steps = kv, kv // CORES

    def q_head(i):
        return lax.rem(hb + 1 + i, kv)

    def kv_pair(i):
        return lax.rem(y + 1 + i, ny)

    def load_wq(i, slot):
        copy(wq.at[:, pl.ds(pl.multiple_of(q_head(i) * width, width), width)], wbuf.at[slot], wsem.at[slot])

    def load_wkv(i, slot):
        cols = pl.ds(pl.multiple_of(kv_pair(i) * pair, pair), pair)
        copy(wk.at[:, cols], wbuf.at[slot, :, pl.ds(0, pair)], wsem.at[slot])
        copy(wv.at[:, cols], wbuf.at[slot, :, pl.ds(pair, pair)], wsem.at[slot])

    load_wq(0, 0)
    lax.fori_loop(0, cp, greet, 0)
    for i, (_, dst, turned) in enumerate(raw):
        wait(dst, load_sem.at[i])
        turned[...] = jnp.transpose(dst[...], (1, 0, 2))
    pl.semaphore_wait(barrier, cp)

    def scatter(item, src, dst, mine, peer):
        def one(k, _):
            h = lax.rem(mine + k, kv)
            put(item, src.at[h], dst, peer(h))
            return 0

        lax.fori_loop(1, kv, one, 0)
        copy(src.at[mine], dst, recv_sem.at[item])

    c_rows = pl.ds(pl.multiple_of(c * cb, cb), cb)
    scatter(KC, tkb, kc.at[y, x, c_rows, :], hb, peer_y)
    scatter(VC, tvb, vc.at[y, x, c_rows, :], hb, peer_y)
    scatter(KAC, tka, kac.at[ha], ha, peer_x)
    scatter(VAC, tva, vac.at[ha], ha, peer_x)

    right = dev(y, lax.rem(x + 1, nx), c)
    left = dev(y, lax.rem(x + nx - 1, nx), c)
    x_left = lax.rem(x + nx - 1, nx)
    x_right = lax.rem(x + 1, nx)
    x_far = lax.rem(x + nx // 2, nx)
    lo, hi = pl.ds(0, ny // 2), pl.ds(ny // 2, ny // 2)

    def ag_sem(i, step, direction):
        return AG + i * 4 + step * 2 + direction

    def ring_first(i, buf):
        put(ag_sem(i, 0, 0), buf.at[:, x], buf.at[:, x], right)
        put(ag_sem(i, 0, 1), buf.at[:, x], buf.at[:, x], left)

    def ring_second(i, buf):
        wait_in(ag_sem(i, 0, 0), buf.at[:, x_left])
        put(ag_sem(i, 1, 0), buf.at[lo, x_left], buf.at[lo, x_left], right)
        wait_in(ag_sem(i, 0, 1), buf.at[:, x_right])
        put(ag_sem(i, 1, 1), buf.at[hi, x_right], buf.at[hi, x_right], left)

    def ring_last(i, buf):
        wait_in(ag_sem(i, 1, 0), buf.at[lo, x_far])
        wait_in(ag_sem(i, 1, 1), buf.at[hi, x_far])

    def ring_drain(i, buf):
        wait_out(ag_sem(i, 0, 0), buf.at[:, x])
        wait_out(ag_sem(i, 0, 1), buf.at[:, x])
        wait_out(ag_sem(i, 1, 0), buf.at[lo, x])
        wait_out(ag_sem(i, 1, 1), buf.at[hi, x])

    wait(xs, load_sem.at[4])
    b_rows, a_rows = pl.ds(0, tb), pl.ds(tb, ta)
    my_a = pl.ds(pl.multiple_of(me * ta, ta), ta)

    def rope(t):
        t = t.astype(bf).astype(jnp.float32)
        return (t * cosf[...] + pltpu.roll(t, dim // 2, 1) * sinf[...]).astype(bf)

    def project(slot):
        return jnp.dot(xs[...], wbuf[slot], preferred_element_type=jnp.float32)

    def q_step(i, _):
        slot = lax.rem(i, 2)

        @pl.when(i + 1 < q_steps)
        def _():
            load_wq(i + 1, 1 - slot)

        @pl.when(i + 1 == q_steps)
        def _():
            load_wkv(0, 1 - slot)

        wait(wbuf.at[slot], wsem.at[slot])
        h = q_head(i)
        lin = project(slot)
        for g in range(grp):
            cols = slice(g * dim, (g + 1) * dim)
            qsend[h, :, cols] = rope(lin[:, cols])
        give(Q, qsend.at[h, b_rows], qbuf.at[hb], peer_y(h))
        for yy in range(ny):
            give(QA, qsend.at[h, a_rows], qabuf.at[my_a, :], dev(yy, h // CORES, lax.rem(h, CORES)))
        return 0

    def kv_step(i, _):
        slot = lax.rem(q_steps + i, 2)

        @pl.when(i + 1 < kv_steps)
        def _():
            load_wkv(i + 1, 1 - slot)

        wait(wbuf.at[slot], wsem.at[slot])
        p = kv_pair(i)
        lin = project(slot)
        for g in range(CORES):
            cols = slice(g * dim, (g + 1) * dim)
            kvsend[p, :, cols] = rope(lin[:, cols])
        kvsend[p, :, pair:2 * pair] = lin[:, pair:2 * pair].astype(bf)
        out_cols = pl.ds(pl.multiple_of(p * pair, pair), pair)
        for j, (nb, na) in enumerate(((nkb, nka), (nvb, nva))):
            cols = pl.ds(j * pair, pair)
            copy(kvsend.at[p, b_rows, cols], nb.at[:, out_cols], out_sem.at[2 * j])
            copy(kvsend.at[p, a_rows, cols], na.at[:, out_cols], out_sem.at[2 * j + 1])
        n_rows = pl.ds(pl.multiple_of(c * tb, tb), tb)
        s_rows = pl.ds(pl.multiple_of(ha * ta, ta), ta)
        for g in range(CORES):
            for j, (ib, db, ia, da) in enumerate(((KN, kn, KAN, kan), (VN, vn, VAN, van))):
                cols = pl.ds(j * pair + g * dim, dim)
                give(ib, kvsend.at[p, b_rows, cols], db.at[y, x, n_rows, :], dev(p, x, g))
                give(ia, kvsend.at[p, a_rows, cols], da.at[s_rows, :], dev(y, p, g))
        return 0

    lax.fori_loop(0, q_steps // 2, q_step, 0)
    wait_in(KC, kc.at[:, x])
    ring_first(0, kc)
    wait_in(VC, vc.at[:, x])
    ring_first(1, vc)
    lax.fori_loop(q_steps // 2, q_steps, q_step, 0)
    lax.fori_loop(0, kv_steps, kv_step, 0)

    def load_q(src, t0):
        for half in range(2):
            for g in range(grp):
                q_s[half, pl.ds(g * tq, tq), :] = src[pl.ds(t0 + half * tq, tq), pl.ds(g * dim, dim)]

    s_refs, p_refs = (s0, s1), (p0, p1)
    blk = s0.shape[0]

    def scores(t, keys):
        s = qk(keys, q_s[t])
        s_refs[t][...] = s
        return fold(s, jnp.maximum)

    def expo(t, m, l8, top8):
        m_new = jnp.maximum(m, jnp.max(top8, axis=0, keepdims=True))
        alpha = jnp.exp2((m - m_new) * scale2)
        l8 = l8 * alpha
        for r in range(0, blk, 16):
            e = jnp.exp2((s_refs[t][pl.ds(r, 16), :] - m_new) * scale2)
            p_refs[t][pl.ds(r, 16), :] = e.astype(bf)
            l8 = l8 + fold(e, jnp.add)
        return m_new, l8, alpha

    def values(t, vt, alpha, accs):
        accs[t][...] = accs[t][...] * alpha + jnp.dot(vt, p_refs[t][...], preferred_element_type=jnp.float32)

    def two_tiles(n, k_at, v_at, accs, state, masks):
        m0, l0, m1, l1 = state
        p1[...] = jnp.zeros_like(p1)
        t0 = scores(0, k_at(0))
        t1 = scores(1, k_at(0))

        def body(j, carry):
            m0, l0, m1, l1, t0, t1, alpha1 = carry
            values(1, v_at(lax.max(j - 1, 0)), alpha1, accs)
            m0, l0, alpha0 = expo(0, m0, l0, t0)
            t0 = scores(0, k_at(j + 1))
            values(0, v_at(j), alpha0, accs)
            m1, l1, alpha1 = expo(1, m1, l1, t1)
            t1 = scores(1, k_at(j + 1))
            return m0, l0, m1, l1, t0, t1, alpha1

        m0, l0, m1, l1, t0, t1, alpha1 = lax.fori_loop(
            0, n - 1, body, (m0, l0, m1, l1, t0, t1, jnp.ones((1, rows), jnp.float32)))
        values(1, v_at(lax.max(n - 2, 0)), alpha1, accs)
        if masks is not None:
            tops = []
            for t in range(2):
                s = jnp.where(masks[t], s_refs[t][...], NEG)
                s_refs[t][...] = s
                tops.append(fold(s, jnp.maximum))
            t0, t1 = tops
        m0, l0, alpha0 = expo(0, m0, l0, t0)
        values(0, v_at(n - 1), alpha0, accs)
        m1, l1, alpha1 = expo(1, m1, l1, t1)
        values(1, v_at(n - 1), alpha1, accs)
        return m0, l0, m1, l1

    def fresh(accs):
        for a in accs:
            a[...] = jnp.zeros_like(a)
        neg = jnp.full((1, rows), NEG, jnp.float32)
        zero = jnp.zeros((8, rows), jnp.float32)
        return neg, zero, neg, zero

    def total(l8):
        return jnp.sum(l8, axis=0, keepdims=True)

    def token_of_lane(shape):
        return lax.rem(lax.broadcasted_iota(jnp.int32, shape, 1), tq)

    wait_in(QA, qabuf)
    wait_in(KAC, kac)
    wait_in(VAC, vac)
    wait_in(KAN, kan)
    wait_in(VAN, van)

    def turn_a(j, _):
        vtac[j] = vac[j].T
        return 0

    lax.fori_loop(0, kv, turn_a, 0)
    vtan[...] = van[...].T
    new_a = kan.shape[0]

    def unit_a(u, _):
        t0 = pl.multiple_of(u * 2 * tq, 2 * tq)
        load_q(qabuf, t0)
        accs = (acc.at[0], acc.at[1])
        m0, l0, m1, l1 = two_tiles(kv, lambda j: kac[j], lambda j: vtac[j], accs, fresh(accs), None)
        pos_k = y * new_a + lax.broadcasted_iota(jnp.int32, (new_a, rows), 0)
        pos_q = t0 + token_of_lane((new_a, rows))
        out = []
        for half, (m, l) in enumerate(((m0, total(l0)), (m1, total(l1)))):
            s = jnp.where(pos_k <= pos_q + half * tq, qk(kan[...], q_s[half]), NEG)
            out.append(soft_step(scale2, s, vtan[...], m, l, accs[half]))
        for half, (m, l) in enumerate(out):
            r = pl.ds(pl.multiple_of(t0 + half * tq, tq), tq)
            row = lax.broadcasted_iota(jnp.int32, (dim, tq), 0)
            stat = jnp.zeros((dim, tq), jnp.float32)
            for g in range(grp):
                cols = slice(g * tq, (g + 1) * tq)
                oastage[r, pl.ds(g * dim, dim)] = acc[half, :, pl.ds(g * tq, tq)].T
                stat = jnp.where(row == g, m[:, cols], stat)
                stat = jnp.where(row == grp + g, l[:, cols], stat)
            ststage[r, :] = stat.T
        return 0

    lax.fori_loop(0, cp * ta // (2 * tq), unit_a, 0)

    slot = y * kv + ha

    def give_a(k, _):
        d = lax.rem(me + k, cp)
        r = pl.ds(pl.multiple_of(d * ta, ta), ta)
        put(OA, oastage.at[r, :], oarecv.at[slot], d)
        put(ST, ststage.at[r, :], strecv.at[slot], d)
        return 0

    lax.fori_loop(1, cp, give_a, 0)
    copy(oastage.at[my_a, :], oarecv.at[slot], recv_sem.at[OA])
    copy(ststage.at[my_a, :], strecv.at[slot], recv_sem.at[ST])

    ring_second(0, kc)
    ring_second(1, vc)
    wait_in(KN, kn.at[:, x])
    ring_first(2, kn)
    wait_in(VN, vn.at[:, x])
    ring_first(3, vn)
    wait_in(Q, qbuf)
    ring_last(0, kc)
    ring_last(1, vc)

    blocks = vtc.shape[0]
    per_row = blocks // ny
    per_blk = nx // per_row

    def cached(buf, j):
        return buf[j // per_row, pl.ds(lax.rem(j, per_row) * per_blk, per_blk)].reshape(blk, dim)

    def turn_c(j, _):
        vtc[j] = cached(vc, j).T
        return 0

    lax.fori_loop(0, blocks, turn_c, 0)

    def keep(u, state):
        for half in range(2):
            m_all[2 * u + half, 0:1, :] = state[2 * half]
            l_all[2 * u + half] = state[2 * half + 1]

    def unit_c(u, _):
        load_q(qbuf.at[u], 0)
        accs = (acc.at[2 * u], acc.at[2 * u + 1])
        keep(u, two_tiles(blocks, lambda j: cached(kc, j), lambda j: vtc[j], accs, fresh(accs), None))
        return 0

    lax.fori_loop(0, kv // 2, unit_c, 0)
    ring_second(2, kn)
    ring_second(3, vn)
    lax.fori_loop(kv // 2, kv, unit_c, 0)
    ring_last(2, kn)
    ring_last(3, vn)

    def turn_n(j, _):
        vtn[j] = vn[j // nx, lax.rem(j, nx)].T
        return 0

    lax.fori_loop(0, ny * nx, turn_n, 0)

    def unit_n(i, _):
        u = lax.rem(hb + 1 + i, kv)
        yy, cc = u // CORES, lax.rem(u, CORES)
        load_q(qbuf.at[u], 0)
        accs = (acc.at[2 * u], acc.at[2 * u + 1])
        state = (m_all[2 * u, 0:1, :], l_all[2 * u], m_all[2 * u + 1, 0:1, :], l_all[2 * u + 1])
        pos_k = lax.broadcasted_iota(jnp.int32, (blk, rows), 0)
        pos_q = cc * tb + token_of_lane((blk, rows))
        masks = (pos_k <= pos_q, pos_k <= pos_q + tq)
        m0, l0, m1, l1 = two_tiles(
            yy * nx + x + 1, lambda j: kn[j // nx, lax.rem(j, nx)], lambda j: vtn[j], accs, state, masks)
        for half, l in enumerate((l0, l1)):
            inv = 1.0 / total(l)
            for g in range(grp):
                o = acc[2 * u + half, :, pl.ds(g * tq, tq)] * inv[:, g * tq:(g + 1) * tq]
                obuf[u, pl.ds(half * tq, tq), pl.ds(g * dim, dim)] = o.T.astype(bf)
        give(OB, obuf.at[u], ob.at[:, pl.ds(pl.multiple_of(hb * width, width), width)], peer_y(u))
        return 0

    lax.fori_loop(0, kv, unit_n, 0)

    wait_in(OA, oarecv)
    wait_in(ST, strecv)

    def merge_a(h, _):
        for g in range(grp):
            ms = [strecv[i * kv + h, :, g:g + 1] for i in range(ny)]
            ls = [strecv[i * kv + h, :, grp + g:grp + g + 1] for i in range(ny)]
            top = functools.reduce(jnp.maximum, ms)
            num = jnp.zeros((ta, dim), jnp.float32)
            den = jnp.zeros((ta, 1), jnp.float32)
            for i in range(ny):
                w = jnp.exp2((ms[i] - top) * scale2)
                num = num + w * oarecv[i * kv + h, :, pl.ds(g * dim, dim)]
                den = den + w * ls[i]
            oa[:, pl.ds(pl.multiple_of(h * width + g * dim, dim), dim)] = (num / den).astype(bf)
        return 0

    lax.fori_loop(0, kv, merge_a, 0)

    wait_in(OB, ob)
    for i, ref in enumerate((nkb, nka, nvb, nva)):
        wait(ref, out_sem.at[i])
    most = pl.ds(0, kv - 1)
    for item, ref in ((KC, tkb), (VC, tvb), (KAC, tka), (VAC, tva), (Q, qbuf), (OB, obuf)):
        wait_out(item, ref.at[most])
    for item, ref in ((KN, qbuf), (VN, qbuf)):
        wait_out(item, ref.at[most, :, pl.ds(0, dim)])
    for item, ref in ((KAN, kan), (VAN, van)):
        wait_out(item, ref.at[pl.ds(0, (kv - 1) * ta), :])
    wait_out(QA, qabuf.at[pl.ds(0, (cp - 1) * ta), :])
    wait_out(OA, oarecv.at[pl.ds(0, cp - 1)])
    wait_out(ST, strecv.at[pl.ds(0, cp - 1)])
    ring_drain(0, kc)
    ring_drain(1, vc)
    ring_drain(2, kn)
    ring_drain(3, vn)


def attention(cp, xb, xa, cosf, sinf, wq, wk, wv, kcb, vcb, kca, vca):
    kv, dim = kcb.shape[1:]
    ny, nx = kv // CORES, cp // kv
    assert nx * CORES == kv and ny * nx * CORES == cp and ny == nx
    grp = wq.shape[1] // (kv * dim)
    tb, ta, cb, ca, model = xb.shape[0], xa.shape[0], kcb.shape[0], kca.shape[0], xb.shape[1]
    tq = tb // 2
    rows, width = grp * tq, grp * dim
    blk = CORES * tb
    assert blk == ca and (ny * nx * CORES * cb) % (ny * blk) == 0 and (cp * ta) % (2 * tq) == 0
    assert width == 2 * CORES * dim
    bf, f32 = jnp.bfloat16, jnp.float32
    vm = pltpu.VMEM
    scratch = [
        vm((tb + ta, model), bf),
        vm((2, model, width), bf),
        vm((kv, tb + ta, width), bf),
        vm((ny, tb + ta, width), bf),
        vm(kcb.shape, bf), vm(vcb.shape, bf), vm(kca.shape, bf), vm(vca.shape, bf),
        vm((kv, cb, dim), bf), vm((kv, cb, dim), bf), vm((kv, ca, dim), bf), vm((kv, ca, dim), bf),
        vm((kv, tb, width), bf),
        vm((ny, nx, CORES * cb, dim), bf),
        vm((ny, nx, CORES * cb, dim), bf),
        vm((ny, nx, blk, dim), bf),
        vm((ny, nx, blk, dim), bf),
        vm((cp * cb // blk, dim, blk), bf),
        vm((ny * nx, dim, blk), bf),
        vm((kv, tb, width), bf),
        vm((2 * kv, dim, rows), f32),
        vm((2 * kv, 8, rows), f32),
        vm((2 * kv, 8, rows), f32),
        vm((2, rows, dim), bf),
        vm((blk, rows), f32),
        vm((blk, rows), f32),
        vm((blk, rows), bf),
        vm((blk, rows), bf),
        vm((cp * ta, width), bf),
        vm((kv, ca, dim), bf),
        vm((kv, ca, dim), bf),
        vm((kv * ta, dim), bf),
        vm((kv * ta, dim), bf),
        vm((kv, dim, ca), bf),
        vm((dim, kv * ta), bf),
        vm((cp * ta, width), f32),
        vm((cp * ta, dim), f32),
        vm((cp, ta, width), f32),
        vm((cp, ta, dim), f32),
        pltpu.SemaphoreType.DMA((29,)),
        pltpu.SemaphoreType.DMA((29,)),
        pltpu.SemaphoreType.DMA((5,)),
        pltpu.SemaphoreType.DMA((2,)),
        pltpu.SemaphoreType.DMA((4,)),
    ]
    any_spec = pl.BlockSpec(memory_space=pl.ANY)
    vmem_spec = pl.BlockSpec(memory_space=pltpu.VMEM)
    shape = jax.ShapeDtypeStruct
    return pl.pallas_call(
        functools.partial(kernel, (ny, nx, kv, grp, dim)),
        out_shape=(shape((tb, kv * width), bf), shape((ta, kv * width), bf),
                   shape((tb, kv * dim), bf), shape((tb, kv * dim), bf),
                   shape((ta, kv * dim), bf), shape((ta, kv * dim), bf)),
        in_specs=[any_spec, any_spec, vmem_spec, vmem_spec] + [any_spec] * 7,
        out_specs=(any_spec, vmem_spec) + (any_spec,) * 4,
        scratch_shapes=scratch,
        compiler_params=pltpu.CompilerParams(
            collective_id=0, has_side_effects=True, vmem_limit_bytes=VMEM_LIMIT),
        name="attend",
    )(xb, xa, cosf, sinf, wq, wk, wv, kcb, vcb, kca, vca)


def out_kernel(ob, oa, w, yb, ya, o):
    tb = ob.shape[0]

    @pl.when(pl.program_id(0) == 0)
    def _():
        o[pl.ds(0, tb), :] = ob[...]
        o[pl.ds(tb, oa.shape[0]), :] = oa[...]

    out = jnp.dot(o[...], w[...], preferred_element_type=jnp.float32).astype(yb.dtype)
    yb[...] = out[:tb]
    ya[...] = out[tb:]


def output_projection(ob, oa, w):
    (tb, inner), ta, model = ob.shape, oa.shape[0], w.shape[1]
    cols = min(512, model)
    shape = jax.ShapeDtypeStruct
    return pl.pallas_call(
        out_kernel,
        grid=(model // cols,),
        out_shape=(shape((tb, model), ob.dtype), shape((ta, model), ob.dtype)),
        in_specs=[pl.BlockSpec((tb, inner), lambda i: (0, 0)), pl.BlockSpec((ta, inner), lambda i: (0, 0)),
                  pl.BlockSpec((inner, cols), lambda i: (0, i))],
        out_specs=(pl.BlockSpec((tb, cols), lambda i: (0, i)), pl.BlockSpec((ta, cols), lambda i: (0, i))),
        scratch_shapes=[pltpu.VMEM((tb + ta, inner), ob.dtype)],
        compiler_params=pltpu.CompilerParams(vmem_limit_bytes=VMEM_LIMIT),
        name="project_out",
    )(ob, oa, w)


def solution(mesh):
    cp_size = mesh.shape["cp"]

    def local_step(x_a, kc_a, vc_a, x_b, kc_b, vc_b, w_q, w_k, w_v, w_o):
        ta, tb = x_a.shape[0], x_b.shape[0]
        kv, dim = kc_a.shape[1:]
        me = lax.axis_index("cp")
        pos_a = kc_a.shape[0] * cp_size + me * ta + jnp.arange(ta)
        pos_b = kc_b.shape[0] * cp_size + me * tb + jnp.arange(tb)
        cosf, sinf = rope_tables(jnp.concatenate([pos_b, pos_a]), dim)
        o_b, o_a, k_b, v_b, k_a, v_a = attention(cp_size, x_b, x_a, cosf, sinf, w_q, w_k, w_v, kc_b, vc_b, kc_a, vc_a)
        y_b, y_a = output_projection(o_b, o_a, w_o)
        heads = lambda t: t.reshape(t.shape[0], kv, dim)
        return y_a, heads(k_a), heads(v_a), y_b, heads(k_b), heads(v_b)

    row_spec = P(("dp", "cp"), None)
    kv_spec = P(("dp", "cp"), None, None)
    full_spec = P()
    return jax.shard_map(
        local_step, mesh=mesh,
        in_specs=(row_spec, kv_spec, kv_spec, row_spec, kv_spec, kv_spec, full_spec, full_spec, full_spec, full_spec),
        out_specs=(row_spec, kv_spec, kv_spec, row_spec, kv_spec, kv_spec), check_vma=False)
```

time: 266 us -> 220 us (0.83)
  matrix products: 40.6 us -> 0 us
  Pallas kernels: 197 us -> 214 us
  local copies, waits for them, and re-layouts: 18.2 us -> 3.05 us
  other arithmetic: 8.21 us -> 1.44 us
    dot_general x4 -> x0, matrix products: 40.6 us -> none  [the longest x3 24.6 us: proj(): jnp.dot(x, w, preferred_element_type=jnp.float32).astype(jnp.bfloat16)]
    pallas_call x0 -> x1, Pallas kernels: none -> 18 us  [output_projection(): pl.pallas_call(out_kernel, grid=(model // cols,), out_shape=(shape((tb, m...]
    unnamed x33 -> x12, local copies, waits for them, and re-layouts: 13.4 us -> 3.05 us
    another operation x2 -> x0, other arithmetic: 5.98 us -> none
    reshape x2 -> x0, local copies, waits for them, and re-layouts: 2.71 us -> none  [local_step(): flat = lambda t: t.reshape(t.shape[0], kv * dim)]
where the time goes in v2:
time: 220 us; the launch traced here: 219 us
  Pallas kernels  214 us (97%)
  local copies, waits for them, and re-layouts  3.05 us (1%)
    pallas_call x1, Pallas kernels, attention(): pl.pallas_call(functools.partial(kernel, (ny, nx, kv, grp, dim)), out_sha...  196 us
    pallas_call x1, Pallas kernels, output_projection(): pl.pallas_call(out_kernel, grid=(model // cols,), out_shape=(shape((tb, m...  18 us

profile of v2, /device:TPU:103, one launch (start us, length us, event | category | flops | bytes accessed | tf_op | source)
XLA Modules:
  0.0 219.3 jit_solution(16876609009334986827)
XLA Ops:
  0.7 0.6 fusion
  1.3 0.9 pad_maximum_fusion
  2.1 196.1 %attend.1 = (bf16[256,4096]{1,0:T(8,128)(2,1)}, bf16[16,4096]{1,0:T(8,128)(2,1)}, bf16[256,1024]{1,0:T(8,128)(2,1)}, bf16[256,1024]{1,0:T(8,128)(2,1)}, bf16[16,...) custom-call(bf16[256,4096]{1,0:T(8,128)(2,1)} %xb.1, bf16[16,4096]{1,0:T(8,128)(2,1)} %xa.1, ...), custom_call_target="tpu_custom_call" | custom-call | tf_op jit(solution)/shard_map/attend/pallas_call | solution.py:540
  198.2 0.0 copy-start.3
  198.2 0.0 copy-start.2
  198.2 0.0 copy-start.1
  198.2 0.0 copy-start
  198.2 18.0 %project_out.1 = (bf16[256,4096]{1,0:T(8,128)(2,1)}, bf16[16,4096]{1,0:T(8,128)(2,1)}) custom-call(bf16[256,4096]{1,0:T(8,128)(2,1)} %get-tuple-element.14.ob, bf16[16,4096]{1,0:T(8,128)(2,1)} %get-tuple-element.15.oa, bf16[4096,4096]{1,0:T(8,128)(2,1)} %w.1), custom_call_target="tpu_custom_call" | custom-call | tf_op jit(solution)/shard_map/project_out/pallas_call | solution.py:571
  216.2 0.0 copy-done.3
  216.2 0.6 copy.16
  216.9 0.0 copy-done.2
  216.9 0.6 copy.17
  217.5 0.0 copy-done.1
  217.5 0.9 copy.18
  218.4 0.0 copy-done
  218.4 0.9 copy.19
  (4 shorter events, 0.0 us)
Async XLA Ops:
  198.2 18.1 %copy-start.3 = (bf16[16,1024]{1,0:T(8,128)(2,1)S(1)}, bf16[16,1024]{1,0:T(8,128)(2,1)}, u32[]{:S(2)}) copy-start(bf16[16,1024]{1,0:T(8,128)(2,1)} %get-tuple-element.17) | copy-start | bytes 98308
  198.2 18.7 %copy-start.2 = (bf16[16,1024]{1,0:T(8,128)(2,1)S(1)}, bf16[16,1024]{1,0:T(8,128)(2,1)}, u32[]{:S(2)}) copy-start(bf16[16,1024]{1,0:T(8,128)(2,1)} %get-tuple-element.18) | copy-start | bytes 98308
  198.2 19.3 %copy-start.1 = (bf16[256,1024]{1,0:T(8,128)(2,1)S(1)}, bf16[256,1024]{1,0:T(8,128)(2,1)}, u32[]{:S(2)}) copy-start(bf16[256,1024]{1,0:T(8,128)(2,1)} %get-tuple-element.20) | copy-start | bytes 1572868
  198.2 20.2 %copy-start = (bf16[256,1024]{1,0:T(8,128)(2,1)S(1)}, bf16[256,1024]{1,0:T(8,128)(2,1)}, u32[]{:S(2)}) copy-start(bf16[256,1024]{1,0:T(8,128)(2,1)} %get-tuple-element.21) | copy-start | bytes 1572868

commit v3 on v2

--- a/solution.py
+++ b/solution.py
@@ -43,8 +43,8 @@
 
 def kernel(dims, xb, xa, cosf, sinf, wq, wk, wv, kcb, vcb, kca, vca, ob, oa, nkb, nvb, nka, nva,
            xs, wbuf, qsend, kvsend, rkb, rvb, rka, rva, tkb, tvb, tka, tva,
-           qbuf, kc, vc, kn, vn, vtc, vtn, obuf, acc, m_all, l_all, q_s, s0, s1, p0, p1,
-           qabuf, kac, vac, kan, van, vtac, vtan, oastage, ststage, oarecv, strecv,
+           qbuf, kc, vc, kn, vn, vtc, vtn, obuf, acc, m_all, l_all, q_s, q_all, s0, s1, p0, p1,
+           qabuf, kac, vac, kan, van, vtac, vtan, oastage, ststage, oarecv, strecv, odone, accx,
            send_sem, recv_sem, load_sem, wsem, out_sem):
     ny, nx, kv, grp, dim = dims
     cp = ny * nx * CORES
@@ -100,8 +100,8 @@
     def wait_out(item, ref):
         wait(ref, send_sem.at[item])
 
-    KC, VC, Q, KN, VN, KAC, VAC, KAN, VAN, QA, OB, OA, ST = range(13)
-    AG = 13
+    KC, VC, Q, KN, VN, KAC, VAC, KAN, VAN, QA, QY, OB, OA, ST, OX = range(15)
+    AG = 15
 
     barrier = pltpu.get_barrier_semaphore()
 
@@ -151,7 +151,6 @@
     scatter(KC, tkb, kc.at[y, x, c_rows, :], hb, peer_y)
     scatter(VC, tvb, vc.at[y, x, c_rows, :], hb, peer_y)
     scatter(KAC, tka, kac.at[ha], ha, peer_x)
-    scatter(VAC, tva, vac.at[ha], ha, peer_x)
 
     right = dev(y, lax.rem(x + 1, nx), c)
     left = dev(y, lax.rem(x + nx - 1, nx), c)
@@ -212,8 +211,7 @@
             cols = slice(g * dim, (g + 1) * dim)
             qsend[h, :, cols] = rope(lin[:, cols])
         give(Q, qsend.at[h, b_rows], qbuf.at[hb], peer_y(h))
-        for yy in range(ny):
-            give(QA, qsend.at[h, a_rows], qabuf.at[my_a, :], dev(yy, h // CORES, lax.rem(h, CORES)))
+        give(QA, qsend.at[h, a_rows], qabuf.at[my_a, :], peer_x(h))
         return 0
 
     def kv_step(i, _):
@@ -251,6 +249,18 @@
     ring_first(1, vc)
     lax.fori_loop(q_steps // 2, q_steps, q_step, 0)
     lax.fori_loop(0, kv_steps, kv_step, 0)
+    ring_second(0, kc)
+    ring_second(1, vc)
+    scatter(VAC, tva, vac.at[ha], ha, peer_x)
+    new_a = kan.shape[0]
+    row_a = pl.ds(pl.multiple_of(y * new_a, new_a), new_a)
+    wait_in(QA, qabuf.at[row_a, :])
+
+    def pass_qa(k, _):
+        put(QY, qabuf.at[row_a, :], qabuf.at[row_a, :], dev(lax.rem(y + k, ny), x, c))
+        return 0
+
+    lax.fori_loop(1, ny, pass_qa, 0)
 
     def load_q(src, t0):
         for half in range(2):
@@ -260,8 +270,8 @@
     s_refs, p_refs = (s0, s1), (p0, p1)
     blk = s0.shape[0]
 
-    def scores(t, keys):
-        s = qk(keys, q_s[t])
+    def scores(t, keys, queries):
+        s = qk(keys, queries)
         s_refs[t][...] = s
         return fold(s, jnp.maximum)
 
@@ -275,40 +285,26 @@
             l8 = l8 + fold(e, jnp.add)
         return m_new, l8, alpha
 
-    def values(t, vt, alpha, accs):
-        accs[t][...] = accs[t][...] * alpha + jnp.dot(vt, p_refs[t][...], preferred_element_type=jnp.float32)
-
-    def two_tiles(n, k_at, v_at, accs, state, masks):
-        m0, l0, m1, l1 = state
-        p1[...] = jnp.zeros_like(p1)
-        t0 = scores(0, k_at(0))
-        t1 = scores(1, k_at(0))
-
+    def values(t, vt, alpha, acc_ref):
+        acc_ref[...] = acc_ref[...] * alpha + jnp.dot(vt, p_refs[t][...], preferred_element_type=jnp.float32)
+
+    one = jnp.ones((1, rows), jnp.float32)
+
+    def inner(n, k_at, v_at, queries, accs, state, tops):
         def body(j, carry):
             m0, l0, m1, l1, t0, t1, alpha1 = carry
-            values(1, v_at(lax.max(j - 1, 0)), alpha1, accs)
+            values(1, v_at(lax.max(j - 1, 0)), alpha1, accs[1])
             m0, l0, alpha0 = expo(0, m0, l0, t0)
-            t0 = scores(0, k_at(j + 1))
-            values(0, v_at(j), alpha0, accs)
+            t0 = scores(0, k_at(j + 1), queries(0))
+            values(0, v_at(j), alpha0, accs[0])
             m1, l1, alpha1 = expo(1, m1, l1, t1)
-            t1 = scores(1, k_at(j + 1))
+            t1 = scores(1, k_at(j + 1), queries(1))
             return m0, l0, m1, l1, t0, t1, alpha1
 
-        m0, l0, m1, l1, t0, t1, alpha1 = lax.fori_loop(
-            0, n - 1, body, (m0, l0, m1, l1, t0, t1, jnp.ones((1, rows), jnp.float32)))
-        values(1, v_at(lax.max(n - 2, 0)), alpha1, accs)
-        if masks is not None:
-            tops = []
-            for t in range(2):
-                s = jnp.where(masks[t], s_refs[t][...], NEG)
-                s_refs[t][...] = s
-                tops.append(fold(s, jnp.maximum))
-            t0, t1 = tops
-        m0, l0, alpha0 = expo(0, m0, l0, t0)
-        values(0, v_at(n - 1), alpha0, accs)
-        m1, l1, alpha1 = expo(1, m1, l1, t1)
-        values(1, v_at(n - 1), alpha1, accs)
-        return m0, l0, m1, l1
+        p1[...] = jnp.zeros_like(p1)
+        out = lax.fori_loop(0, n - 1, body, state + tops + (one,))
+        values(1, v_at(lax.max(n - 2, 0)), out[6], accs[1])
+        return out[:4], out[4:6]
 
     def fresh(accs):
         for a in accs:
@@ -323,7 +319,70 @@
     def token_of_lane(shape):
         return lax.rem(lax.broadcasted_iota(jnp.int32, shape, 1), tq)
 
-    wait_in(QA, qabuf)
+    wait_in(Q, qbuf)
+
+    def tiles_q(u, _):
+        for half in range(2):
+            for g in range(grp):
+                q_all[2 * u + half, pl.ds(g * tq, tq), :] = qbuf[u, pl.ds(half * tq, tq), pl.ds(g * dim, dim)]
+        return 0
+
+    lax.fori_loop(0, kv, tiles_q, 0)
+    ring_last(0, kc)
+    ring_last(1, vc)
+
+    blocks = vtc.shape[0]
+    per_row = blocks // ny
+    per_blk = nx // per_row
+
+    def cached(buf, j):
+        return buf[j // per_row, pl.ds(lax.rem(j, per_row) * per_blk, per_blk)].reshape(blk, dim)
+
+    def turn_c(j, _):
+        vtc[j] = cached(vc, j).T
+        return 0
+
+    lax.fori_loop(0, blocks, turn_c, 0)
+    acc[...] = jnp.zeros_like(acc)
+    p1[...] = jnp.zeros_like(p1)
+    steps = kv * blocks
+
+    def step_c(t, carry):
+        m0, l0, m1, l1, t0, t1, alpha1 = carry
+        u, j = t // blocks, lax.rem(t, blocks)
+        before, after = lax.max(t - 1, 0), lax.min(t + 1, steps - 1)
+        u_after, k_after = after // blocks, cached(kc, lax.rem(after, blocks))
+        values(1, vtc[lax.rem(before, blocks)], alpha1, acc.at[2 * (before // blocks) + 1])
+        m0, m1 = jnp.where(j == 0, NEG, m0), jnp.where(j == 0, NEG, m1)
+        l0, l1 = jnp.where(j == 0, 0.0, l0), jnp.where(j == 0, 0.0, l1)
+        m0, l0, alpha0 = expo(0, m0, l0, t0)
+        t0 = scores(0, k_after, q_all[2 * u_after])
+        values(0, vtc[j], alpha0, acc.at[2 * u])
+        m1, l1, alpha1 = expo(1, m1, l1, t1)
+        t1 = scores(1, k_after, q_all[2 * u_after + 1])
+        m_all[2 * u, 0:1, :] = m0
+        m_all[2 * u + 1, 0:1, :] = m1
+        l_all[2 * u] = l0
+        l_all[2 * u + 1] = l1
+        return m0, l0, m1, l1, t0, t1, alpha1
+
+    neg, zero = jnp.full((1, rows), NEG, jnp.float32), jnp.zeros((8, rows), jnp.float32)
+    carry = (neg, zero, neg, zero, scores(0, cached(kc, 0), q_all[0]), scores(1, cached(kc, 0), q_all[1]), one)
+    carry = lax.fori_loop(0, steps // 4, step_c, carry)
+    wait_in(KN, kn.at[:, x])
+    ring_first(2, kn)
+    wait_in(VN, vn.at[:, x])
+    ring_first(3, vn)
+    carry = lax.fori_loop(steps // 4, steps - steps // 8, step_c, carry)
+    ring_second(2, kn)
+    ring_second(3, vn)
+    carry = lax.fori_loop(steps - steps // 8, steps, step_c, carry)
+    values(1, vtc[blocks - 1], carry[6], acc.at[2 * kv - 1])
+
+    def other_rows(ref):
+        return ref.at[pl.ds(0, (ny - 1) * new_a), :]
+
+    wait_in(QY, other_rows(qabuf))
     wait_in(KAC, kac)
     wait_in(VAC, vac)
     wait_in(KAN, kan)
@@ -335,26 +394,28 @@
 
     lax.fori_loop(0, kv, turn_a, 0)
     vtan[...] = van[...].T
-    new_a = kan.shape[0]
+    acc_a = (accx.at[0], accx.at[1])
 
     def unit_a(u, _):
         t0 = pl.multiple_of(u * 2 * tq, 2 * tq)
         load_q(qabuf, t0)
-        accs = (acc.at[0], acc.at[1])
-        m0, l0, m1, l1 = two_tiles(kv, lambda j: kac[j], lambda j: vtac[j], accs, fresh(accs), None)
+        tops = scores(0, kac[0], q_s[0]), scores(1, kac[0], q_s[1])
+        state, tops = inner(kv, lambda j: kac[j], lambda j: vtac[j], lambda t: q_s[t], acc_a, fresh(acc_a), tops)
         pos_k = y * new_a + lax.broadcasted_iota(jnp.int32, (new_a, rows), 0)
         pos_q = t0 + token_of_lane((new_a, rows))
         out = []
-        for half, (m, l) in enumerate(((m0, total(l0)), (m1, total(l1)))):
+        for half in range(2):
+            m, l, alpha = expo(half, state[2 * half], state[2 * half + 1], tops[half])
+            values(half, vtac[kv - 1], alpha, acc_a[half])
             s = jnp.where(pos_k <= pos_q + half * tq, qk(kan[...], q_s[half]), NEG)
-            out.append(soft_step(scale2, s, vtan[...], m, l, accs[half]))
+            out.append(soft_step(scale2, s, vtan[...], m, total(l), acc_a[half]))
         for half, (m, l) in enumerate(out):
             r = pl.ds(pl.multiple_of(t0 + half * tq, tq), tq)
             row = lax.broadcasted_iota(jnp.int32, (dim, tq), 0)
             stat = jnp.zeros((dim, tq), jnp.float32)
             for g in range(grp):
                 cols = slice(g * tq, (g + 1) * tq)
-                oastage[r, pl.ds(g * dim, dim)] = acc[half, :, pl.ds(g * tq, tq)].T
+                oastage[r, pl.ds(g * dim, dim)] = accx[half, :, pl.ds(g * tq, tq)].T
                 stat = jnp.where(row == g, m[:, cols], stat)
                 stat = jnp.where(row == grp + g, l[:, cols], stat)
             ststage[r, :] = stat.T
@@ -362,57 +423,17 @@
 
     lax.fori_loop(0, cp * ta // (2 * tq), unit_a, 0)
 
-    slot = y * kv + ha
-
     def give_a(k, _):
-        d = lax.rem(me + k, cp)
-        r = pl.ds(pl.multiple_of(d * ta, ta), ta)
-        put(OA, oastage.at[r, :], oarecv.at[slot], d)
-        put(ST, ststage.at[r, :], strecv.at[slot], d)
-        return 0
-
-    lax.fori_loop(1, cp, give_a, 0)
-    copy(oastage.at[my_a, :], oarecv.at[slot], recv_sem.at[OA])
-    copy(ststage.at[my_a, :], strecv.at[slot], recv_sem.at[ST])
-
-    ring_second(0, kc)
-    ring_second(1, vc)
-    wait_in(KN, kn.at[:, x])
-    ring_first(2, kn)
-    wait_in(VN, vn.at[:, x])
-    ring_first(3, vn)
-    wait_in(Q, qbuf)
-    ring_last(0, kc)
-    ring_last(1, vc)
-
-    blocks = vtc.shape[0]
-    per_row = blocks // ny
-    per_blk = nx // per_row
-
-    def cached(buf, j):
-        return buf[j // per_row, pl.ds(lax.rem(j, per_row) * per_blk, per_blk)].reshape(blk, dim)
-
-    def turn_c(j, _):
-        vtc[j] = cached(vc, j).T
-        return 0
-
-    lax.fori_loop(0, blocks, turn_c, 0)
-
-    def keep(u, state):
-        for half in range(2):
-            m_all[2 * u + half, 0:1, :] = state[2 * half]
-            l_all[2 * u + half] = state[2 * half + 1]
-
-    def unit_c(u, _):
-        load_q(qbuf.at[u], 0)
-        accs = (acc.at[2 * u], acc.at[2 * u + 1])
-        keep(u, two_tiles(blocks, lambda j: cached(kc, j), lambda j: vtc[j], accs, fresh(accs), None))
-        return 0
-
-    lax.fori_loop(0, kv // 2, unit_c, 0)
-    ring_second(2, kn)
-    ring_second(3, vn)
-    lax.fori_loop(kv // 2, kv, unit_c, 0)
+        yy = lax.rem(y + k, ny)
+        r = pl.ds(pl.multiple_of(yy * new_a, new_a), new_a)
+        put(OA, oastage.at[r, :], oarecv.at[y], dev(yy, x, c))
+        put(ST, ststage.at[r, :], strecv.at[y], dev(yy, x, c))
+        return 0
+
+    lax.fori_loop(1, ny, give_a, 0)
+    copy(oastage.at[row_a, :], oarecv.at[y], recv_sem.at[OA])
+    copy(ststage.at[row_a, :], strecv.at[y], recv_sem.at[ST])
+
     ring_last(2, kn)
     ring_last(3, vn)
 
@@ -422,47 +443,63 @@
 
     lax.fori_loop(0, ny * nx, turn_n, 0)
 
-    def unit_n(i, _):
-        u = lax.rem(hb + 1 + i, kv)
+    def new_keys(j):
+        return kn[j // nx, lax.rem(j, nx)]
+
+    def unit_of(i):
+        return lax.rem(hb + 1 + i, kv)
+
+    def unit_n(i, tops):
+        u, u_after = unit_of(i), unit_of(lax.min(i + 1, kv - 1))
         yy, cc = u // CORES, lax.rem(u, CORES)
-        load_q(qbuf.at[u], 0)
+        last = yy * nx + x
         accs = (acc.at[2 * u], acc.at[2 * u + 1])
         state = (m_all[2 * u, 0:1, :], l_all[2 * u], m_all[2 * u + 1, 0:1, :], l_all[2 * u + 1])
+        state, _ = inner(last + 1, new_keys, lambda j: vtn[j], lambda t: q_all[2 * u + t], accs, state, tops)
         pos_k = lax.broadcasted_iota(jnp.int32, (blk, rows), 0)
         pos_q = cc * tb + token_of_lane((blk, rows))
-        masks = (pos_k <= pos_q, pos_k <= pos_q + tq)
-        m0, l0, m1, l1 = two_tiles(
-            yy * nx + x + 1, lambda j: kn[j // nx, lax.rem(j, nx)], lambda j: vtn[j], accs, state, masks)
-        for half, l in enumerate((l0, l1)):
+        tops = []
+        for half in range(2):
+            s = jnp.where(pos_k <= pos_q + half * tq, s_refs[half][...], NEG)
+            s_refs[half][...] = s
+            m, l, alpha = expo(half, state[2 * half], state[2 * half + 1], fold(s, jnp.maximum))
+            tops.append(scores(half, new_keys(0), q_all[2 * u_after + half]))
+            values(half, vtn[last], alpha, accs[half])
             inv = 1.0 / total(l)
             for g in range(grp):
                 o = acc[2 * u + half, :, pl.ds(g * tq, tq)] * inv[:, g * tq:(g + 1) * tq]
                 obuf[u, pl.ds(half * tq, tq), pl.ds(g * dim, dim)] = o.T.astype(bf)
         give(OB, obuf.at[u], ob.at[:, pl.ds(pl.multiple_of(hb * width, width), width)], peer_y(u))
-        return 0
-
-    lax.fori_loop(0, kv, unit_n, 0)
+        return tuple(tops)
+
+    u = unit_of(0)
+    tops = scores(0, new_keys(0), q_all[2 * u]), scores(1, new_keys(0), q_all[2 * u + 1])
+    tops = lax.fori_loop(0, kv - 2, unit_n, tops)
 
     wait_in(OA, oarecv)
     wait_in(ST, strecv)
-
-    def merge_a(h, _):
-        for g in range(grp):
-            ms = [strecv[i * kv + h, :, g:g + 1] for i in range(ny)]
-            ls = [strecv[i * kv + h, :, grp + g:grp + g + 1] for i in range(ny)]
-            top = functools.reduce(jnp.maximum, ms)
-            num = jnp.zeros((ta, dim), jnp.float32)
-            den = jnp.zeros((ta, 1), jnp.float32)
-            for i in range(ny):
-                w = jnp.exp2((ms[i] - top) * scale2)
-                num = num + w * oarecv[i * kv + h, :, pl.ds(g * dim, dim)]
-                den = den + w * ls[i]
-            oa[:, pl.ds(pl.multiple_of(h * width + g * dim, dim), dim)] = (num / den).astype(bf)
-        return 0
-
-    lax.fori_loop(0, kv, merge_a, 0)
+    for g in range(grp):
+        cols = pl.ds(g * dim, dim)
+        ms = [strecv[i, :, g:g + 1] for i in range(ny)]
+        top = functools.reduce(jnp.maximum, ms)
+        num = jnp.zeros((new_a, dim), jnp.float32)
+        den = jnp.zeros((new_a, 1), jnp.float32)
+        for i in range(ny):
+            w = jnp.exp2((ms[i] - top) * scale2)
+            num = num + w * oarecv[i, :, cols]
+            den = den + w * strecv[i, :, grp + g:grp + g + 1]
+        odone[:, cols] = (num / den).astype(bf)
+
+    def home_a(r, _):
+        give(OX, odone.at[pl.ds(pl.multiple_of(r * ta, ta), ta), :],
+             oa.at[:, pl.ds(pl.multiple_of(ha * width, width), width)], peer_x(r))
+        return 0
+
+    lax.fori_loop(0, kv, home_a, 0)
+    lax.fori_loop(kv - 2, kv, unit_n, tops)
 
     wait_in(OB, ob)
+    wait_in(OX, oa)
     for i, ref in enumerate((nkb, nka, nvb, nva)):
         wait(ref, out_sem.at[i])
     most = pl.ds(0, kv - 1)
@@ -472,9 +509,11 @@
         wait_out(item, ref.at[most, :, pl.ds(0, dim)])
     for item, ref in ((KAN, kan), (VAN, van)):
         wait_out(item, ref.at[pl.ds(0, (kv - 1) * ta), :])
-    wait_out(QA, qabuf.at[pl.ds(0, (cp - 1) * ta), :])
-    wait_out(OA, oarecv.at[pl.ds(0, cp - 1)])
-    wait_out(ST, strecv.at[pl.ds(0, cp - 1)])
+    wait_out(QA, qabuf.at[pl.ds(0, (kv - 1) * ta), :])
+    wait_out(OX, odone.at[pl.ds(0, (kv - 1) * ta), :])
+    wait_out(QY, other_rows(qabuf))
+    wait_out(OA, oarecv.at[pl.ds(0, ny - 1)])
+    wait_out(ST, strecv.at[pl.ds(0, ny - 1)])
     ring_drain(0, kc)
     ring_drain(1, vc)
     ring_drain(2, kn)
@@ -513,6 +552,7 @@
         vm((2 * kv, 8, rows), f32),
         vm((2 * kv, 8, rows), f32),
         vm((2, rows, dim), bf),
+        vm((2 * kv, rows, dim), bf),
         vm((blk, rows), f32),
         vm((blk, rows), f32),
         vm((blk, rows), bf),
@@ -526,10 +566,12 @@
         vm((dim, kv * ta), bf),
         vm((cp * ta, width), f32),
         vm((cp * ta, dim), f32),
-        vm((cp, ta, width), f32),
-        vm((cp, ta, dim), f32),
-        pltpu.SemaphoreType.DMA((29,)),
-        pltpu.SemaphoreType.DMA((29,)),
+        vm((ny, kv * ta, width), f32),
+        vm((ny, kv * ta, dim), f32),
+        vm((kv * ta, width), bf),
+        vm((2, dim, rows), f32),
+        pltpu.SemaphoreType.DMA((31,)),
+        pltpu.SemaphoreType.DMA((31,)),
         pltpu.SemaphoreType.DMA((5,)),
         pltpu.SemaphoreType.DMA((2,)),
         pltpu.SemaphoreType.DMA((4,)),
@@ -543,7 +585,7 @@
                    shape((tb, kv * dim), bf), shape((tb, kv * dim), bf),
                    shape((ta, kv * dim), bf), shape((ta, kv * dim), bf)),
         in_specs=[any_spec, any_spec, vmem_spec, vmem_spec] + [any_spec] * 7,
-        out_specs=(any_spec, vmem_spec) + (any_spec,) * 4,
+        out_specs=(any_spec,) * 6,
         scratch_shapes=scratch,
         compiler_params=pltpu.CompilerParams(
             collective_id=0, has_side_effects=True, vmem_limit_bytes=VMEM_LIMIT),

time: 220 us -> 180 us (0.82)
  Pallas kernels: 214 us -> 173 us
    pallas_call x1, Pallas kernels: 196 us -> 155 us  [attention(): pl.pallas_call(functools.partial(kernel, (ny, nx, kv, grp, dim)), out_sha...]
where the time goes in v3:
time: 180 us; the launch traced here: 178 us
  Pallas kernels  173 us (96%)
  local copies, waits for them, and re-layouts  3.05 us (2%)
    pallas_call x1, Pallas kernels, attention(): pl.pallas_call(functools.partial(kernel, (ny, nx, kv, grp, dim)), out_sha...  155 us
    pallas_call x1, Pallas kernels, output_projection(): pl.pallas_call(out_kernel, grid=(model // cols,), out_shape=(shape((tb, m...  18 us

profile of v3, /device:TPU:103, one launch (start us, length us, event | category | flops | bytes accessed | tf_op | source)
XLA Modules:
  0.0 178.1 jit_solution(16373796459721423264)
XLA Ops:
  0.7 0.6 fusion
  1.3 0.9 pad_maximum_fusion
  2.1 154.9 %attend.1 = (bf16[256,4096]{1,0:T(8,128)(2,1)}, bf16[16,4096]{1,0:T(8,128)(2,1)}, bf16[256,1024]{1,0:T(8,128)(2,1)}, bf16[256,1024]{1,0:T(8,128)(2,1)}, bf16[16,...) custom-call(bf16[256,4096]{1,0:T(8,128)(2,1)} %xb.1, bf16[16,4096]{1,0:T(8,128)(2,1)} %xa.1, ...), custom_call_target="tpu_custom_call" | custom-call | tf_op jit(solution)/shard_map/attend/pallas_call | solution.py:582
  157.0 0.0 copy-start.3
  157.0 0.0 copy-start.2
  157.0 0.0 copy-start.1
  157.1 0.0 copy-start
  157.1 18.0 %project_out.1 = (bf16[256,4096]{1,0:T(8,128)(2,1)}, bf16[16,4096]{1,0:T(8,128)(2,1)}) custom-call(bf16[256,4096]{1,0:T(8,128)(2,1)} %get-tuple-element.14.ob, bf16[16,4096]{1,0:T(8,128)(2,1)} %get-tuple-element.15.oa, bf16[4096,4096]{1,0:T(8,128)(2,1)} %w.1), custom_call_target="tpu_custom_call" | custom-call | tf_op jit(solution)/shard_map/project_out/pallas_call | solution.py:613
  175.1 0.0 copy-done.3
  175.1 0.6 copy.16
  175.7 0.0 copy-done.2
  175.7 0.6 copy.17
  176.3 0.0 copy-done.1
  176.3 0.9 copy.18
  177.2 0.0 copy-done
  177.2 0.9 copy.19
  (4 shorter events, 0.0 us)
Async XLA Ops:
  157.0 18.1 %copy-start.3 = (bf16[16,1024]{1,0:T(8,128)(2,1)S(1)}, bf16[16,1024]{1,0:T(8,128)(2,1)}, u32[]{:S(2)}) copy-start(bf16[16,1024]{1,0:T(8,128)(2,1)} %get-tuple-element.17) | copy-start | bytes 98308
  157.0 18.7 %copy-start.2 = (bf16[16,1024]{1,0:T(8,128)(2,1)S(1)}, bf16[16,1024]{1,0:T(8,128)(2,1)}, u32[]{:S(2)}) copy-start(bf16[16,1024]{1,0:T(8,128)(2,1)} %get-tuple-element.18) | copy-start | bytes 98308
  157.0 19.3 %copy-start.1 = (bf16[256,1024]{1,0:T(8,128)(2,1)S(1)}, bf16[256,1024]{1,0:T(8,128)(2,1)}, u32[]{:S(2)}) copy-start(bf16[256,1024]{1,0:T(8,128)(2,1)} %get-tuple-element.20) | copy-start | bytes 1572868
  157.1 20.2 %copy-start = (bf16[256,1024]{1,0:T(8,128)(2,1)S(1)}, bf16[256,1024]{1,0:T(8,128)(2,1)}, u32[]{:S(2)}) copy-start(bf16[256,1024]{1,0:T(8,128)(2,1)} %get-tuple-element.21) | copy-start | bytes 1572868

commit v4 on v3

--- a/solution.py
+++ b/solution.py
@@ -43,8 +43,8 @@
 
 def kernel(dims, xb, xa, cosf, sinf, wq, wk, wv, kcb, vcb, kca, vca, ob, oa, nkb, nvb, nka, nva,
            xs, wbuf, qsend, kvsend, rkb, rvb, rka, rva, tkb, tvb, tka, tva,
-           qbuf, kc, vc, kn, vn, vtc, vtn, obuf, acc, m_all, l_all, q_s, q_all, s0, s1, p0, p1,
-           qabuf, kac, vac, kan, van, vtac, vtan, oastage, ststage, oarecv, strecv, odone, accx,
+           qbuf, kc, vc, kn, vn, vtc, vtn, obuf, acc, m_all, l_all, q_a, q_all, s0, s1, s2, s3, p0, p1, p2, p3,
+           qabuf, kac, vac, kan, van, vtac, vtan, oastage, ststage, oarecv, strecv, odone, acc_a,
            send_sem, recv_sem, load_sem, wsem, out_sem):
     ny, nx, kv, grp, dim = dims
     cp = ny * nx * CORES
@@ -101,7 +101,8 @@
         wait(ref, send_sem.at[item])
 
     KC, VC, Q, KN, VN, KAC, VAC, KAN, VAN, QA, QY, OB, OA, ST, OX = range(15)
-    AG = 15
+    QS = 15
+    AG = QS + ny
 
     barrier = pltpu.get_barrier_semaphore()
 
@@ -150,7 +151,6 @@
     c_rows = pl.ds(pl.multiple_of(c * cb, cb), cb)
     scatter(KC, tkb, kc.at[y, x, c_rows, :], hb, peer_y)
     scatter(VC, tvb, vc.at[y, x, c_rows, :], hb, peer_y)
-    scatter(KAC, tka, kac.at[ha], ha, peer_x)
 
     right = dev(y, lax.rem(x + 1, nx), c)
     left = dev(y, lax.rem(x + nx - 1, nx), c)
@@ -210,7 +210,7 @@
         for g in range(grp):
             cols = slice(g * dim, (g + 1) * dim)
             qsend[h, :, cols] = rope(lin[:, cols])
-        give(Q, qsend.at[h, b_rows], qbuf.at[hb], peer_y(h))
+        give(QS + lax.rem(y - h // CORES + ny, ny), qsend.at[h, b_rows], qbuf.at[hb], peer_y(h))
         give(QA, qsend.at[h, a_rows], qabuf.at[my_a, :], peer_x(h))
         return 0
 
@@ -228,11 +228,11 @@
             cols = slice(g * dim, (g + 1) * dim)
             kvsend[p, :, cols] = rope(lin[:, cols])
         kvsend[p, :, pair:2 * pair] = lin[:, pair:2 * pair].astype(bf)
-        out_cols = pl.ds(pl.multiple_of(p * pair, pair), pair)
         for j, (nb, na) in enumerate(((nkb, nka), (nvb, nva))):
-            cols = pl.ds(j * pair, pair)
-            copy(kvsend.at[p, b_rows, cols], nb.at[:, out_cols], out_sem.at[2 * j])
-            copy(kvsend.at[p, a_rows, cols], na.at[:, out_cols], out_sem.at[2 * j + 1])
+            for g in range(CORES):
+                cols = pl.ds(j * pair + g * dim, dim)
+                copy(kvsend.at[p, b_rows, cols], nb.at[p * CORES + g], out_sem.at[2 * j])
+                copy(kvsend.at[p, a_rows, cols], na.at[p * CORES + g], out_sem.at[2 * j + 1])
         n_rows = pl.ds(pl.multiple_of(c * tb, tb), tb)
         s_rows = pl.ds(pl.multiple_of(ha * ta, ta), ta)
         for g in range(CORES):
@@ -248,9 +248,10 @@
     wait_in(VC, vc.at[:, x])
     ring_first(1, vc)
     lax.fori_loop(q_steps // 2, q_steps, q_step, 0)
-    lax.fori_loop(0, kv_steps, kv_step, 0)
     ring_second(0, kc)
     ring_second(1, vc)
+    scatter(KAC, tka, kac.at[ha], ha, peer_x)
+    lax.fori_loop(0, kv_steps, kv_step, 0)
     scatter(VAC, tva, vac.at[ha], ha, peer_x)
     new_a = kan.shape[0]
     row_a = pl.ds(pl.multiple_of(y * new_a, new_a), new_a)
@@ -262,22 +263,21 @@
 
     lax.fori_loop(1, ny, pass_qa, 0)
 
-    def load_q(src, t0):
-        for half in range(2):
-            for g in range(grp):
-                q_s[half, pl.ds(g * tq, tq), :] = src[pl.ds(t0 + half * tq, tq), pl.ds(g * dim, dim)]
-
-    s_refs, p_refs = (s0, s1), (p0, p1)
+    s_refs, p_refs = (s0, s1, s2, s3), (p0, p1, p2, p3)
     blk = s0.shape[0]
+    tiles = range(4)
 
     def scores(t, keys, queries):
         s = qk(keys, queries)
         s_refs[t][...] = s
         return fold(s, jnp.maximum)
 
+    def highest(m, top8):
+        m_new = jnp.maximum(m, jnp.max(top8, axis=0, keepdims=True))
+        return m_new, jnp.exp2((m - m_new) * scale2)
+
     def expo(t, m, l8, top8):
-        m_new = jnp.maximum(m, jnp.max(top8, axis=0, keepdims=True))
-        alpha = jnp.exp2((m - m_new) * scale2)
+        m_new, alpha = highest(m, top8)
         l8 = l8 * alpha
         for r in range(0, blk, 16):
             e = jnp.exp2((s_refs[t][pl.ds(r, 16), :] - m_new) * scale2)
@@ -288,30 +288,18 @@
     def values(t, vt, alpha, acc_ref):
         acc_ref[...] = acc_ref[...] * alpha + jnp.dot(vt, p_refs[t][...], preferred_element_type=jnp.float32)
 
+    def step(carry, before, now, k_after, q_after, acc_before, accs):
+        m, l, top = list(carry[0:4]), list(carry[4:8]), list(carry[8:12])
+        values(3, before, carry[12], acc_before)
+        for t in tiles:
+            m[t], l[t], alpha = expo(t, m[t], l[t], top[t])
+            top[t] = scores(t, k_after, q_after(t))
+            if t < 3:
+                values(t, now, alpha, accs[t])
+        return tuple(m + l + top) + (alpha,)
+
+    neg, zero = jnp.full((1, rows), NEG, jnp.float32), jnp.zeros((8, rows), jnp.float32)
     one = jnp.ones((1, rows), jnp.float32)
-
-    def inner(n, k_at, v_at, queries, accs, state, tops):
-        def body(j, carry):
-            m0, l0, m1, l1, t0, t1, alpha1 = carry
-            values(1, v_at(lax.max(j - 1, 0)), alpha1, accs[1])
-            m0, l0, alpha0 = expo(0, m0, l0, t0)
-            t0 = scores(0, k_at(j + 1), queries(0))
-            values(0, v_at(j), alpha0, accs[0])
-            m1, l1, alpha1 = expo(1, m1, l1, t1)
-            t1 = scores(1, k_at(j + 1), queries(1))
-            return m0, l0, m1, l1, t0, t1, alpha1
-
-        p1[...] = jnp.zeros_like(p1)
-        out = lax.fori_loop(0, n - 1, body, state + tops + (one,))
-        values(1, v_at(lax.max(n - 2, 0)), out[6], accs[1])
-        return out[:4], out[4:6]
-
-    def fresh(accs):
-        for a in accs:
-            a[...] = jnp.zeros_like(a)
-        neg = jnp.full((1, rows), NEG, jnp.float32)
-        zero = jnp.zeros((8, rows), jnp.float32)
-        return neg, zero, neg, zero
 
     def total(l8):
         return jnp.sum(l8, axis=0, keepdims=True)
@@ -319,65 +307,70 @@
     def token_of_lane(shape):
         return lax.rem(lax.broadcasted_iota(jnp.int32, shape, 1), tq)
 
-    wait_in(Q, qbuf)
-
-    def tiles_q(u, _):
-        for half in range(2):
-            for g in range(grp):
-                q_all[2 * u + half, pl.ds(g * tq, tq), :] = qbuf[u, pl.ds(half * tq, tq), pl.ds(g * dim, dim)]
-        return 0
-
-    lax.fori_loop(0, kv, tiles_q, 0)
-    ring_last(0, kc)
-    ring_last(1, vc)
+    def turn(n, dst, block):
+        def four(i, _):
+            for k in range(4):
+                dst[4 * i + k] = block(4 * i + k).T
+            return 0
+
+        lax.fori_loop(0, n // 4, four, 0)
 
     blocks = vtc.shape[0]
     per_row = blocks // ny
     per_blk = nx // per_row
+    acc[...] = jnp.zeros_like(acc)
+    p3[...] = jnp.zeros_like(p3)
+
+    def row_of(i):
+        return lax.rem(y + i, ny)
+
+    def arrive_q(i):
+        yy = row_of(i)
+        wait_in(QS + i, qbuf.at[pl.ds(yy * CORES, CORES)])
+        for t in tiles:
+            u, half = yy * CORES + t // 2, t % 2
+            for g in range(grp):
+                q_all[4 * yy + t, pl.ds(g * tq, tq), :] = qbuf[u, pl.ds(half * tq, tq), pl.ds(g * dim, dim)]
 
     def cached(buf, j):
         return buf[j // per_row, pl.ds(lax.rem(j, per_row) * per_blk, per_blk)].reshape(blk, dim)
 
-    def turn_c(j, _):
-        vtc[j] = cached(vc, j).T
-        return 0
-
-    lax.fori_loop(0, blocks, turn_c, 0)
-    acc[...] = jnp.zeros_like(acc)
-    p1[...] = jnp.zeros_like(p1)
-    steps = kv * blocks
-
-    def step_c(t, carry):
-        m0, l0, m1, l1, t0, t1, alpha1 = carry
-        u, j = t // blocks, lax.rem(t, blocks)
-        before, after = lax.max(t - 1, 0), lax.min(t + 1, steps - 1)
-        u_after, k_after = after // blocks, cached(kc, lax.rem(after, blocks))
-        values(1, vtc[lax.rem(before, blocks)], alpha1, acc.at[2 * (before // blocks) + 1])
-        m0, m1 = jnp.where(j == 0, NEG, m0), jnp.where(j == 0, NEG, m1)
-        l0, l1 = jnp.where(j == 0, 0.0, l0), jnp.where(j == 0, 0.0, l1)
-        m0, l0, alpha0 = expo(0, m0, l0, t0)
-        t0 = scores(0, k_after, q_all[2 * u_after])
-        values(0, vtc[j], alpha0, acc.at[2 * u])
-        m1, l1, alpha1 = expo(1, m1, l1, t1)
-        t1 = scores(1, k_after, q_all[2 * u_after + 1])
-        m_all[2 * u, 0:1, :] = m0
-        m_all[2 * u + 1, 0:1, :] = m1
-        l_all[2 * u] = l0
-        l_all[2 * u + 1] = l1
-        return m0, l0, m1, l1, t0, t1, alpha1
-
-    neg, zero = jnp.full((1, rows), NEG, jnp.float32), jnp.zeros((8, rows), jnp.float32)
-    carry = (neg, zero, neg, zero, scores(0, cached(kc, 0), q_all[0]), scores(1, cached(kc, 0), q_all[1]), one)
-    carry = lax.fori_loop(0, steps // 4, step_c, carry)
+    arrive_q(0)
+    ring_last(0, kc)
+    ring_last(1, vc)
+    turn(blocks, vtc, lambda j: cached(vc, j))
+
+    def step_c(i, carry):
+        yy, j = row_of(i // blocks), lax.rem(i, blocks)
+        before, after = lax.max(i - 1, 0), lax.min(i + 1, ny * blocks - 1)
+        y_before, y_after = row_of(before // blocks), row_of(after // blocks)
+        start = j == 0
+        m = tuple(jnp.where(start, NEG, v) for v in carry[0:4])
+        l = tuple(jnp.where(start, 0.0, v) for v in carry[4:8])
+        out = step(
+            m + l + carry[8:], vtc[lax.rem(before, blocks)], vtc[j], cached(kc, lax.rem(after, blocks)),
+            lambda t: q_all[4 * y_after + t], acc.at[4 * y_before + 3], [acc.at[4 * yy + t] for t in tiles])
+        for t in tiles:
+            m_all[4 * yy + t, 0:1, :] = out[t]
+            l_all[4 * yy + t] = out[4 + t]
+        return out
+
+    tops = tuple(scores(t, cached(kc, 0), q_all[4 * y + t]) for t in tiles)
+    carry = (neg,) * 4 + (zero,) * 4 + tops + (one,)
+    carry = lax.fori_loop(0, blocks - 1, step_c, carry)
+    arrive_q(1)
+    carry = lax.fori_loop(blocks - 1, 2 * blocks - 1, step_c, carry)
     wait_in(KN, kn.at[:, x])
     ring_first(2, kn)
     wait_in(VN, vn.at[:, x])
     ring_first(3, vn)
-    carry = lax.fori_loop(steps // 4, steps - steps // 8, step_c, carry)
+    arrive_q(2)
+    carry = lax.fori_loop(2 * blocks - 1, 3 * blocks - 1, step_c, carry)
+    arrive_q(3)
+    carry = lax.fori_loop(3 * blocks - 1, 4 * blocks, step_c, carry)
     ring_second(2, kn)
     ring_second(3, vn)
-    carry = lax.fori_loop(steps - steps // 8, steps, step_c, carry)
-    values(1, vtc[blocks - 1], carry[6], acc.at[2 * kv - 1])
+    values(3, vtc[blocks - 1], carry[12], acc.at[4 * row_of(ny - 1) + 3])
 
     def other_rows(ref):
         return ref.at[pl.ds(0, (ny - 1) * new_a), :]
@@ -387,41 +380,36 @@
     wait_in(VAC, vac)
     wait_in(KAN, kan)
     wait_in(VAN, van)
-
-    def turn_a(j, _):
-        vtac[j] = vac[j].T
-        return 0
-
-    lax.fori_loop(0, kv, turn_a, 0)
+    turn(kv, vtac, lambda j: vac[j])
     vtan[...] = van[...].T
-    acc_a = (accx.at[0], accx.at[1])
-
-    def unit_a(u, _):
-        t0 = pl.multiple_of(u * 2 * tq, 2 * tq)
-        load_q(qabuf, t0)
-        tops = scores(0, kac[0], q_s[0]), scores(1, kac[0], q_s[1])
-        state, tops = inner(kv, lambda j: kac[j], lambda j: vtac[j], lambda t: q_s[t], acc_a, fresh(acc_a), tops)
-        pos_k = y * new_a + lax.broadcasted_iota(jnp.int32, (new_a, rows), 0)
-        pos_q = t0 + token_of_lane((new_a, rows))
-        out = []
-        for half in range(2):
-            m, l, alpha = expo(half, state[2 * half], state[2 * half + 1], tops[half])
-            values(half, vtac[kv - 1], alpha, acc_a[half])
-            s = jnp.where(pos_k <= pos_q + half * tq, qk(kan[...], q_s[half]), NEG)
-            out.append(soft_step(scale2, s, vtan[...], m, total(l), acc_a[half]))
-        for half, (m, l) in enumerate(out):
-            r = pl.ds(pl.multiple_of(t0 + half * tq, tq), tq)
-            row = lax.broadcasted_iota(jnp.int32, (dim, tq), 0)
-            stat = jnp.zeros((dim, tq), jnp.float32)
-            for g in range(grp):
-                cols = slice(g * tq, (g + 1) * tq)
-                oastage[r, pl.ds(g * dim, dim)] = accx[half, :, pl.ds(g * tq, tq)].T
-                stat = jnp.where(row == g, m[:, cols], stat)
-                stat = jnp.where(row == grp + g, l[:, cols], stat)
-            ststage[r, :] = stat.T
-        return 0
-
-    lax.fori_loop(0, cp * ta // (2 * tq), unit_a, 0)
+    for t in tiles:
+        for g in range(grp):
+            q_a[t, pl.ds(g * tq, tq), :] = qabuf[pl.ds(t * tq, tq), pl.ds(g * dim, dim)]
+    acc_a[...] = jnp.zeros_like(acc_a)
+    p3[...] = jnp.zeros_like(p3)
+    accs_a = [acc_a.at[t] for t in tiles]
+
+    def step_a(j, carry):
+        return step(carry, vtac[lax.max(j - 1, 0)], vtac[j], kac[j + 1], lambda t: q_a[t], accs_a[3], accs_a)
+
+    tops = tuple(scores(t, kac[0], q_a[t]) for t in tiles)
+    carry = lax.fori_loop(0, kv - 1, step_a, (neg,) * 4 + (zero,) * 4 + tops + (one,))
+    values(3, vtac[kv - 2], carry[12], accs_a[3])
+    pos_k = y * new_a + lax.broadcasted_iota(jnp.int32, (new_a, rows), 0)
+    pos_q = token_of_lane((new_a, rows))
+    row = lax.broadcasted_iota(jnp.int32, (dim, tq), 0)
+    for t in tiles:
+        m, l, alpha = expo(t, carry[t], carry[4 + t], carry[8 + t])
+        values(t, vtac[kv - 1], alpha, accs_a[t])
+        s = jnp.where(pos_k <= pos_q + t * tq, qk(kan[...], q_a[t]), NEG)
+        m, l = soft_step(scale2, s, vtan[...], m, total(l), accs_a[t])
+        stat = jnp.zeros((dim, tq), jnp.float32)
+        for g in range(grp):
+            cols = slice(g * tq, (g + 1) * tq)
+            oastage[pl.ds(t * tq, tq), pl.ds(g * dim, dim)] = acc_a[t, :, cols].T
+            stat = jnp.where(row == g, m[:, cols], stat)
+            stat = jnp.where(row == grp + g, l[:, cols], stat)
+        ststage[pl.ds(t * tq, tq), :] = stat.T
 
     def give_a(k, _):
         yy = lax.rem(y + k, ny)
@@ -436,45 +424,52 @@
 
     ring_last(2, kn)
     ring_last(3, vn)
-
-    def turn_n(j, _):
-        vtn[j] = vn[j // nx, lax.rem(j, nx)].T
-        return 0
-
-    lax.fori_loop(0, ny * nx, turn_n, 0)
+    turn(ny * nx, vtn, lambda j: vn[j // nx, lax.rem(j, nx)])
 
     def new_keys(j):
         return kn[j // nx, lax.rem(j, nx)]
 
-    def unit_of(i):
-        return lax.rem(hb + 1 + i, kv)
-
-    def unit_n(i, tops):
-        u, u_after = unit_of(i), unit_of(lax.min(i + 1, kv - 1))
-        yy, cc = u // CORES, lax.rem(u, CORES)
+    def rows_n(i, tops):
+        yy, y_after = row_of(1 + i), row_of(lax.min(2 + i, ny))
         last = yy * nx + x
-        accs = (acc.at[2 * u], acc.at[2 * u + 1])
-        state = (m_all[2 * u, 0:1, :], l_all[2 * u], m_all[2 * u + 1, 0:1, :], l_all[2 * u + 1])
-        state, _ = inner(last + 1, new_keys, lambda j: vtn[j], lambda t: q_all[2 * u + t], accs, state, tops)
-        pos_k = lax.broadcasted_iota(jnp.int32, (blk, rows), 0)
-        pos_q = cc * tb + token_of_lane((blk, rows))
+        accs = [acc.at[4 * yy + t] for t in tiles]
+        p3[...] = jnp.zeros_like(p3)
+
+        def step_n(j, carry):
+            return step(carry, vtn[lax.max(j - 1, 0)], vtn[j], new_keys(j + 1), lambda t: q_all[4 * yy + t],
+                        accs[3], accs)
+
+        state = tuple(m_all[4 * yy + t, 0:1, :] for t in tiles) + tuple(l_all[4 * yy + t] for t in tiles)
+        carry = lax.fori_loop(0, last, step_n, state + tuple(tops) + (one,))
+        values(3, vtn[lax.max(last - 1, 0)], carry[12], accs[3])
         tops = []
-        for half in range(2):
-            s = jnp.where(pos_k <= pos_q + half * tq, s_refs[half][...], NEG)
-            s_refs[half][...] = s
-            m, l, alpha = expo(half, state[2 * half], state[2 * half + 1], fold(s, jnp.maximum))
-            tops.append(scores(half, new_keys(0), q_all[2 * u_after + half]))
-            values(half, vtn[last], alpha, accs[half])
-            inv = 1.0 / total(l)
+        for t in tiles:
+            seen = (t + 1) * tq
+            tri = lax.broadcasted_iota(jnp.int32, (tq, rows), 0) <= token_of_lane((tq, rows))
+            s = jnp.where(tri, s_refs[t][pl.ds(t * tq, tq), :], NEG)
+            s_refs[t][pl.ds(t * tq, tq), :] = s
+            top8 = fold(s, jnp.maximum)
+            if t:
+                top8 = jnp.maximum(top8, fold(s_refs[t][pl.ds(0, t * tq), :], jnp.maximum))
+            m_new, alpha = highest(carry[t], top8)
+            l8 = carry[4 + t] * alpha
+            for r in range(0, seen, 16):
+                e = jnp.exp2((s_refs[t][pl.ds(r, 16), :] - m_new) * scale2)
+                p_refs[t][pl.ds(r, 16), :] = e.astype(bf)
+                l8 = l8 + fold(e, jnp.add)
+            tops.append(scores(t, new_keys(0), q_all[4 * y_after + t]))
+            pv = jnp.dot(vtn[last, :, pl.ds(0, seen)], p_refs[t][pl.ds(0, seen), :], preferred_element_type=jnp.float32)
+            o = (accs[t][...] * alpha + pv) * (1.0 / total(l8))
             for g in range(grp):
-                o = acc[2 * u + half, :, pl.ds(g * tq, tq)] * inv[:, g * tq:(g + 1) * tq]
-                obuf[u, pl.ds(half * tq, tq), pl.ds(g * dim, dim)] = o.T.astype(bf)
-        give(OB, obuf.at[u], ob.at[:, pl.ds(pl.multiple_of(hb * width, width), width)], peer_y(u))
+                obuf[yy * CORES + t // 2, pl.ds(t % 2 * tq, tq), pl.ds(g * dim, dim)] = (
+                    o[:, g * tq:(g + 1) * tq].T.astype(bf))
+        for cc in range(CORES):
+            u = yy * CORES + cc
+            give(OB, obuf.at[u], ob.at[:, pl.ds(pl.multiple_of(hb * width, width), width)], peer_y(u))
         return tuple(tops)
 
-    u = unit_of(0)
-    tops = scores(0, new_keys(0), q_all[2 * u]), scores(1, new_keys(0), q_all[2 * u + 1])
-    tops = lax.fori_loop(0, kv - 2, unit_n, tops)
+    tops = tuple(scores(t, new_keys(0), q_all[4 * row_of(1) + t]) for t in tiles)
+    tops = lax.fori_loop(0, ny - 1, rows_n, tops)
 
     wait_in(OA, oarecv)
     wait_in(ST, strecv)
@@ -496,15 +491,18 @@
         return 0
 
     lax.fori_loop(0, kv, home_a, 0)
-    lax.fori_loop(kv - 2, kv, unit_n, tops)
+    lax.fori_loop(ny - 1, ny, rows_n, tops)
 
     wait_in(OB, ob)
     wait_in(OX, oa)
     for i, ref in enumerate((nkb, nka, nvb, nva)):
         wait(ref, out_sem.at[i])
     most = pl.ds(0, kv - 1)
-    for item, ref in ((KC, tkb), (VC, tvb), (KAC, tka), (VAC, tva), (Q, qbuf), (OB, obuf)):
+    for item, ref in ((KC, tkb), (VC, tvb), (KAC, tka), (VAC, tva), (OB, obuf)):
         wait_out(item, ref.at[most])
+    wait_out(QS, qbuf.at[pl.ds(0, CORES - 1)])
+    for i in range(1, ny):
+        wait_out(QS + i, qbuf.at[pl.ds(0, CORES)])
     for item, ref in ((KN, qbuf), (VN, qbuf)):
         wait_out(item, ref.at[most, :, pl.ds(0, dim)])
     for item, ref in ((KAN, kan), (VAN, van)):
@@ -530,7 +528,7 @@
     rows, width = grp * tq, grp * dim
     blk = CORES * tb
     assert blk == ca and (ny * nx * CORES * cb) % (ny * blk) == 0 and (cp * ta) % (2 * tq) == 0
-    assert width == 2 * CORES * dim
+    assert width == 2 * CORES * dim and cp * ta == 4 * tq and CORES == 2
     bf, f32 = jnp.bfloat16, jnp.float32
     vm = pltpu.VMEM
     scratch = [
@@ -551,12 +549,10 @@
         vm((2 * kv, dim, rows), f32),
         vm((2 * kv, 8, rows), f32),
         vm((2 * kv, 8, rows), f32),
-        vm((2, rows, dim), bf),
+        vm((4, rows, dim), bf),
         vm((2 * kv, rows, dim), bf),
-        vm((blk, rows), f32),
-        vm((blk, rows), f32),
-        vm((blk, rows), bf),
-        vm((blk, rows), bf),
+        vm((blk, rows), f32), vm((blk, rows), f32), vm((blk, rows), f32), vm((blk, rows), f32),
+        vm((blk, rows), bf), vm((blk, rows), bf), vm((blk, rows), bf), vm((blk, rows), bf),
         vm((cp * ta, width), bf),
         vm((kv, ca, dim), bf),
         vm((kv, ca, dim), bf),
@@ -569,9 +565,9 @@
         vm((ny, kv * ta, width), f32),
         vm((ny, kv * ta, dim), f32),
         vm((kv * ta, width), bf),
-        vm((2, dim, rows), f32),
-        pltpu.SemaphoreType.DMA((31,)),
-        pltpu.SemaphoreType.DMA((31,)),
+        vm((4, dim, rows), f32),
+        pltpu.SemaphoreType.DMA((15 + ny + 16,)),
+        pltpu.SemaphoreType.DMA((15 + ny + 16,)),
         pltpu.SemaphoreType.DMA((5,)),
         pltpu.SemaphoreType.DMA((2,)),
         pltpu.SemaphoreType.DMA((4,)),
@@ -582,8 +578,8 @@
     return pl.pallas_call(
         functools.partial(kernel, (ny, nx, kv, grp, dim)),
         out_shape=(shape((tb, kv * width), bf), shape((ta, kv * width), bf),
-                   shape((tb, kv * dim), bf), shape((tb, kv * dim), bf),
-                   shape((ta, kv * dim), bf), shape((ta, kv * dim), bf)),
+                   shape((kv, tb, dim), bf), shape((kv, tb, dim), bf),
+                   shape((kv, ta, dim), bf), shape((kv, ta, dim), bf)),
         in_specs=[any_spec, any_spec, vmem_spec, vmem_spec] + [any_spec] * 7,
         out_specs=(any_spec,) * 6,
         scratch_shapes=scratch,
@@ -593,34 +589,76 @@
     )(xb, xa, cosf, sinf, wq, wk, wv, kcb, vcb, kca, vca)
 
 
-def out_kernel(ob, oa, w, yb, ya, o):
-    tb = ob.shape[0]
-
-    @pl.when(pl.program_id(0) == 0)
-    def _():
-        o[pl.ds(0, tb), :] = ob[...]
-        o[pl.ds(tb, oa.shape[0]), :] = oa[...]
-
-    out = jnp.dot(o[...], w[...], preferred_element_type=jnp.float32).astype(yb.dtype)
-    yb[...] = out[:tb]
-    ya[...] = out[tb:]
-
-
-def output_projection(ob, oa, w):
+SLOTS = 3
+
+
+def out_kernel(ob, oa, w, kb, vb, ka, va, yb, ya, nkb, nvb, nka, nva, o, wbuf, ybuf, *rest):
+    new, turned, (wsem, osem, nsem, ysem) = rest[:4], rest[4:8], rest[8:]
+    tb, ta = ob.shape[0], oa.shape[0]
+    cols = wbuf.shape[2]
+    steps = w.shape[1] // cols
+    b_rows, a_rows = pl.ds(0, tb), pl.ds(tb, ta)
+
+    def copy(src, dst, sem):
+        pltpu.make_async_copy(src, dst, sem).start()
+
+    def wait(ref, sem):
+        pltpu.make_async_copy(ref, ref, sem).wait()
+
+    def span(i):
+        return pl.ds(pl.multiple_of(i * cols, cols), cols)
+
+    def load(i):
+        copy(w.at[:, span(i)], wbuf.at[lax.rem(i, SLOTS)], wsem.at[lax.rem(i, SLOTS)])
+
+    copy(ob, o.at[b_rows, :], osem)
+    copy(oa, o.at[a_rows, :], osem)
+    for i in range(min(SLOTS - 1, steps)):
+        load(i)
+    for i, (src, dst) in enumerate(zip((kb, vb, ka, va), new)):
+        copy(src, dst, nsem.at[i])
+    wait(o, osem)
+
+    def step(i, _):
+        @pl.when(i + SLOTS - 1 < steps)
+        def _():
+            load(i + SLOTS - 1)
+
+        slot = lax.rem(i, SLOTS)
+        wait(wbuf.at[slot], wsem.at[slot])
+        ybuf[i] = jnp.dot(o[...], wbuf[slot], preferred_element_type=jnp.float32).astype(ybuf.dtype)
+        copy(ybuf.at[i, b_rows, :], yb.at[:, span(i)], ysem.at[0])
+        copy(ybuf.at[i, a_rows, :], ya.at[:, span(i)], ysem.at[1])
+        return 0
+
+    lax.fori_loop(0, steps, step, 0)
+    for i, (src, dst, out) in enumerate(zip(new, turned, (nkb, nvb, nka, nva))):
+        wait(src, nsem.at[i])
+        dst[...] = jnp.transpose(src[...], (1, 0, 2))
+        copy(dst, out, nsem.at[i])
+    wait(yb, ysem.at[0])
+    wait(ya, ysem.at[1])
+    for i, out in enumerate((nkb, nvb, nka, nva)):
+        wait(out, nsem.at[i])
+
+
+def output_projection(ob, oa, w, *new):
     (tb, inner), ta, model = ob.shape, oa.shape[0], w.shape[1]
     cols = min(512, model)
     shape = jax.ShapeDtypeStruct
+    bf, vm, dma = ob.dtype, pltpu.VMEM, pltpu.SemaphoreType.DMA
+    turned = [(t.shape[1], t.shape[0], t.shape[2]) for t in new]
+    any_spec = pl.BlockSpec(memory_space=pl.ANY)
     return pl.pallas_call(
         out_kernel,
-        grid=(model // cols,),
-        out_shape=(shape((tb, model), ob.dtype), shape((ta, model), ob.dtype)),
-        in_specs=[pl.BlockSpec((tb, inner), lambda i: (0, 0)), pl.BlockSpec((ta, inner), lambda i: (0, 0)),
-                  pl.BlockSpec((inner, cols), lambda i: (0, i))],
-        out_specs=(pl.BlockSpec((tb, cols), lambda i: (0, i)), pl.BlockSpec((ta, cols), lambda i: (0, i))),
-        scratch_shapes=[pltpu.VMEM((tb + ta, inner), ob.dtype)],
+        out_shape=[shape((tb, model), bf), shape((ta, model), bf)] + [shape(t, bf) for t in turned],
+        in_specs=[any_spec] * 7,
+        out_specs=[any_spec] * 6,
+        scratch_shapes=[vm((tb + ta, inner), bf), vm((SLOTS, inner, cols), bf), vm((model // cols, tb + ta, cols), bf)]
+        + [vm(t.shape, bf) for t in new] + [vm(t, bf) for t in turned] + [dma((SLOTS,)), dma, dma((4,)), dma((2,))],
         compiler_params=pltpu.CompilerParams(vmem_limit_bytes=VMEM_LIMIT),
         name="project_out",
-    )(ob, oa, w)
+    )(ob, oa, w, *new)
 
 
 def solution(mesh):
@@ -634,9 +672,8 @@
         pos_b = kc_b.shape[0] * cp_size + me * tb + jnp.arange(tb)
         cosf, sinf = rope_tables(jnp.concatenate([pos_b, pos_a]), dim)
         o_b, o_a, k_b, v_b, k_a, v_a = attention(cp_size, x_b, x_a, cosf, sinf, w_q, w_k, w_v, kc_b, vc_b, kc_a, vc_a)
-        y_b, y_a = output_projection(o_b, o_a, w_o)
-        heads = lambda t: t.reshape(t.shape[0], kv, dim)
-        return y_a, heads(k_a), heads(v_a), y_b, heads(k_b), heads(v_b)
+        y_b, y_a, k_b, v_b, k_a, v_a = output_projection(o_b, o_a, w_o, k_b, v_b, k_a, v_a)
+        return y_a, k_a, v_a, y_b, k_b, v_b
 
     row_spec = P(("dp", "cp"), None)
     kv_spec = P(("dp", "cp"), None, None)

time: 180 us -> 169 us (0.939)
  Pallas kernels: 173 us -> 166 us
  local copies, waits for them, and re-layouts: 3.05 us -> 0 us
    pallas_call x1, Pallas kernels: 155 us -> 151 us  [attention(): pl.pallas_call(functools.partial(kernel, (ny, nx, kv, grp, dim)), out_sha...]
    unnamed x12 -> x0, local copies, waits for them, and re-layouts: 3.05 us -> none
    pallas_call x1, Pallas kernels: 18 us -> 15 us  [output_projection(): pl.pallas_call(out_kernel, out_shape=[shape((tb, model), bf), shape((ta,...]
where the time goes in v4:
time: 169 us; the launch traced here: 168 us
  Pallas kernels  166 us (98%)
    pallas_call x1, Pallas kernels, attention(): pl.pallas_call(functools.partial(kernel, (ny, nx, kv, grp, dim)), out_sha...  151 us
    pallas_call x1, Pallas kernels, output_projection(): pl.pallas_call(out_kernel, out_shape=[shape((tb, model), bf), shape((ta,...  15 us

profile of v4, /device:TPU:103, one launch (start us, length us, event | category | flops | bytes accessed | tf_op | source)
XLA Modules:
  0.0 168.4 jit_solution(13786909871728523417)
XLA Ops:
  0.7 0.6 fusion
  1.3 0.9 pad_maximum_fusion
  2.1 151.1 %attend.1 = (bf16[256,4096]{1,0:T(8,128)(2,1)}, bf16[16,4096]{1,0:T(8,128)(2,1)}, bf16[8,256,128]{2,1,0:T(8,128)(2,1)}, bf16[8,256,128]{2,1,0:T(8,128)(2,1)}, bf...) custom-call(bf16[256,4096]{1,0:T(8,128)(2,1)} %xb.1, bf16[16,4096]{1,0:T(8,128)(2,1)} %xa.1, ...), custom_call_target="tpu_custom_call" | custom-call | tf_op jit(solution)/shard_map/attend/pallas_call | solution.py:578
  153.2 15.0 %project_out.1 = (bf16[256,4096]{1,0:T(8,128)(2,1)}, bf16[16,4096]{1,0:T(8,128)(2,1)}, bf16[256,8,128]{2,1,0:T(8,128)(2,1)}, bf16[256,8,128]{2,1,0:T(8,128)(2,1)...) custom-call(bf16[256,4096]{1,0:T(8,128)(2,1)} %get-tuple-element.18.ob, ...), custom_call_target="tpu_custom_call" | custom-call | tf_op jit(solution)/shard_map/project_out/pallas_call | solution.py:652
  (4 shorter events, 0.0 us)

commit v5 on v4

--- a/solution.py
+++ b/solution.py
@@ -13,6 +13,7 @@
 MESH = pl.DeviceIdType.MESH
 CORES = 2
 VMEM_LIMIT = 62 * 1024 * 1024
+SLOTS = 3
 
 
 def rope_tables(positions, head_dim):
@@ -61,17 +62,13 @@
     c = lax.rem(me, CORES)
     x = lax.rem(me // CORES, nx)
     y = me // (CORES * nx)
-    hb = y * CORES + c
-    ha = x * CORES + c
+    mine = y * CORES + c
 
     def dev(yy, xx, cc):
         return (yy * nx + xx) * CORES + cc
 
-    def peer_y(h):
+    def peer(h):
         return dev(h // CORES, x, lax.rem(h, CORES))
-
-    def peer_x(h):
-        return dev(y, h // CORES, lax.rem(h, CORES))
 
     def put(item, src, dst, target):
         pltpu.make_async_remote_copy(
@@ -100,7 +97,7 @@
     def wait_out(item, ref):
         wait(ref, send_sem.at[item])
 
-    KC, VC, Q, KN, VN, KAC, VAC, KAN, VAN, QA, QY, OB, OA, ST, OX = range(15)
+    KC, VC, Q, KN, VN, KAC, VAC, KAN, VAN, QA, QX, OB, OA, ST, OY = range(15)
     QS = 15
     AG = QS + ny
 
@@ -119,27 +116,39 @@
     q_steps, kv_steps = kv, kv // CORES
 
     def q_head(i):
-        return lax.rem(hb + 1 + i, kv)
+        return lax.rem(mine + 1 + i, kv)
 
     def kv_pair(i):
         return lax.rem(y + 1 + i, ny)
 
-    def load_wq(i, slot):
+    def load_q_cols(i, slot):
         copy(wq.at[:, pl.ds(pl.multiple_of(q_head(i) * width, width), width)], wbuf.at[slot], wsem.at[slot])
 
-    def load_wkv(i, slot):
+    def load_kv_cols(i, slot):
         cols = pl.ds(pl.multiple_of(kv_pair(i) * pair, pair), pair)
         copy(wk.at[:, cols], wbuf.at[slot, :, pl.ds(0, pair)], wsem.at[slot])
         copy(wv.at[:, cols], wbuf.at[slot, :, pl.ds(pair, pair)], wsem.at[slot])
 
-    load_wq(0, 0)
+    def load_cols(i):
+        slot = lax.rem(i, SLOTS)
+
+        @pl.when(i < kv_steps)
+        def _():
+            load_kv_cols(i, slot)
+
+        @pl.when(jnp.logical_and(i >= kv_steps, i < kv_steps + q_steps))
+        def _():
+            load_q_cols(i - kv_steps, slot)
+
+    for i in range(SLOTS - 1):
+        load_cols(jnp.int32(i))
     lax.fori_loop(0, cp, greet, 0)
     for i, (_, dst, turned) in enumerate(raw):
         wait(dst, load_sem.at[i])
         turned[...] = jnp.transpose(dst[...], (1, 0, 2))
     pl.semaphore_wait(barrier, cp)
 
-    def scatter(item, src, dst, mine, peer):
+    def scatter(item, src, dst):
         def one(k, _):
             h = lax.rem(mine + k, kv)
             put(item, src.at[h], dst, peer(h))
@@ -149,8 +158,8 @@
         copy(src.at[mine], dst, recv_sem.at[item])
 
     c_rows = pl.ds(pl.multiple_of(c * cb, cb), cb)
-    scatter(KC, tkb, kc.at[y, x, c_rows, :], hb, peer_y)
-    scatter(VC, tvb, vc.at[y, x, c_rows, :], hb, peer_y)
+    scatter(KC, tkb, kc.at[y, x, c_rows, :])
+    scatter(VC, tvb, vc.at[y, x, c_rows, :])
 
     right = dev(y, lax.rem(x + 1, nx), c)
     left = dev(y, lax.rem(x + nx - 1, nx), c)
@@ -184,7 +193,9 @@
 
     wait(xs, load_sem.at[4])
     b_rows, a_rows = pl.ds(0, tb), pl.ds(tb, ta)
-    my_a = pl.ds(pl.multiple_of(me * ta, ta), ta)
+    new_a = kv * ta
+    col_a = pl.ds(pl.multiple_of(x * new_a, new_a), new_a)
+    my_a = pl.ds(pl.multiple_of(x * new_a + mine * ta, ta), ta)
 
     def rope(t):
         t = t.astype(bf).astype(jnp.float32)
@@ -194,33 +205,21 @@
         return jnp.dot(xs[...], wbuf[slot], preferred_element_type=jnp.float32)
 
     def q_step(i, _):
-        slot = lax.rem(i, 2)
-
-        @pl.when(i + 1 < q_steps)
-        def _():
-            load_wq(i + 1, 1 - slot)
-
-        @pl.when(i + 1 == q_steps)
-        def _():
-            load_wkv(0, 1 - slot)
-
+        load_cols(kv_steps + i + SLOTS - 1)
+        slot = lax.rem(kv_steps + i, SLOTS)
         wait(wbuf.at[slot], wsem.at[slot])
         h = q_head(i)
         lin = project(slot)
         for g in range(grp):
             cols = slice(g * dim, (g + 1) * dim)
             qsend[h, :, cols] = rope(lin[:, cols])
-        give(QS + lax.rem(y - h // CORES + ny, ny), qsend.at[h, b_rows], qbuf.at[hb], peer_y(h))
-        give(QA, qsend.at[h, a_rows], qabuf.at[my_a, :], peer_x(h))
+        give(QS + lax.rem(y - h // CORES + ny, ny), qsend.at[h, b_rows], qbuf.at[mine], peer(h))
+        give(QA, qsend.at[h, a_rows], qabuf.at[my_a, :], peer(h))
         return 0
 
     def kv_step(i, _):
-        slot = lax.rem(q_steps + i, 2)
-
-        @pl.when(i + 1 < kv_steps)
-        def _():
-            load_wkv(i + 1, 1 - slot)
-
+        load_cols(i + SLOTS - 1)
+        slot = lax.rem(i, SLOTS)
         wait(wbuf.at[slot], wsem.at[slot])
         p = kv_pair(i)
         lin = project(slot)
@@ -234,34 +233,29 @@
                 copy(kvsend.at[p, b_rows, cols], nb.at[p * CORES + g], out_sem.at[2 * j])
                 copy(kvsend.at[p, a_rows, cols], na.at[p * CORES + g], out_sem.at[2 * j + 1])
         n_rows = pl.ds(pl.multiple_of(c * tb, tb), tb)
-        s_rows = pl.ds(pl.multiple_of(ha * ta, ta), ta)
+        s_rows = pl.ds(pl.multiple_of(mine * ta, ta), ta)
         for g in range(CORES):
             for j, (ib, db, ia, da) in enumerate(((KN, kn, KAN, kan), (VN, vn, VAN, van))):
                 cols = pl.ds(j * pair + g * dim, dim)
                 give(ib, kvsend.at[p, b_rows, cols], db.at[y, x, n_rows, :], dev(p, x, g))
-                give(ia, kvsend.at[p, a_rows, cols], da.at[s_rows, :], dev(y, p, g))
+                give(ia, kvsend.at[p, a_rows, cols], da.at[s_rows, :], dev(p, x, g))
         return 0
 
-    lax.fori_loop(0, q_steps // 2, q_step, 0)
+    lax.fori_loop(0, kv_steps, kv_step, 0)
     wait_in(KC, kc.at[:, x])
     ring_first(0, kc)
     wait_in(VC, vc.at[:, x])
     ring_first(1, vc)
-    lax.fori_loop(q_steps // 2, q_steps, q_step, 0)
+    lax.fori_loop(0, q_steps - 1, q_step, 0)
     ring_second(0, kc)
     ring_second(1, vc)
-    scatter(KAC, tka, kac.at[ha], ha, peer_x)
-    lax.fori_loop(0, kv_steps, kv_step, 0)
-    scatter(VAC, tva, vac.at[ha], ha, peer_x)
-    new_a = kan.shape[0]
-    row_a = pl.ds(pl.multiple_of(y * new_a, new_a), new_a)
-    wait_in(QA, qabuf.at[row_a, :])
-
-    def pass_qa(k, _):
-        put(QY, qabuf.at[row_a, :], qabuf.at[row_a, :], dev(lax.rem(y + k, ny), x, c))
-        return 0
-
-    lax.fori_loop(1, ny, pass_qa, 0)
+    lax.fori_loop(q_steps - 1, q_steps, q_step, 0)
+    wait_in(KN, kn.at[:, x])
+    ring_first(2, kn)
+    wait_in(VN, vn.at[:, x])
+    ring_first(3, vn)
+    scatter(KAC, tka, kac.at[mine])
+    scatter(VAC, tva, vac.at[mine])
 
     s_refs, p_refs = (s0, s1, s2, s3), (p0, p1, p2, p3)
     blk = s0.shape[0]
@@ -303,6 +297,9 @@
 
     def total(l8):
         return jnp.sum(l8, axis=0, keepdims=True)
+
+    def others(ref):
+        return ref.at[pl.ds(0, (nx - 1) * new_a), :]
 
     def token_of_lane(shape):
         return lax.rem(lax.broadcasted_iota(jnp.int32, shape, 1), tq)
@@ -360,67 +357,20 @@
     carry = lax.fori_loop(0, blocks - 1, step_c, carry)
     arrive_q(1)
     carry = lax.fori_loop(blocks - 1, 2 * blocks - 1, step_c, carry)
-    wait_in(KN, kn.at[:, x])
-    ring_first(2, kn)
-    wait_in(VN, vn.at[:, x])
-    ring_first(3, vn)
+    wait_in(QA, qabuf.at[col_a, :])
+
+    def pass_qa(k, _):
+        put(QX, qabuf.at[col_a, :], qabuf.at[col_a, :], dev(y, lax.rem(x + k, nx), c))
+        return 0
+
+    lax.fori_loop(1, nx, pass_qa, 0)
     arrive_q(2)
     carry = lax.fori_loop(2 * blocks - 1, 3 * blocks - 1, step_c, carry)
     arrive_q(3)
-    carry = lax.fori_loop(3 * blocks - 1, 4 * blocks, step_c, carry)
     ring_second(2, kn)
     ring_second(3, vn)
+    carry = lax.fori_loop(3 * blocks - 1, 4 * blocks, step_c, carry)
     values(3, vtc[blocks - 1], carry[12], acc.at[4 * row_of(ny - 1) + 3])
-
-    def other_rows(ref):
-        return ref.at[pl.ds(0, (ny - 1) * new_a), :]
-
-    wait_in(QY, other_rows(qabuf))
-    wait_in(KAC, kac)
-    wait_in(VAC, vac)
-    wait_in(KAN, kan)
-    wait_in(VAN, van)
-    turn(kv, vtac, lambda j: vac[j])
-    vtan[...] = van[...].T
-    for t in tiles:
-        for g in range(grp):
-            q_a[t, pl.ds(g * tq, tq), :] = qabuf[pl.ds(t * tq, tq), pl.ds(g * dim, dim)]
-    acc_a[...] = jnp.zeros_like(acc_a)
-    p3[...] = jnp.zeros_like(p3)
-    accs_a = [acc_a.at[t] for t in tiles]
-
-    def step_a(j, carry):
-        return step(carry, vtac[lax.max(j - 1, 0)], vtac[j], kac[j + 1], lambda t: q_a[t], accs_a[3], accs_a)
-
-    tops = tuple(scores(t, kac[0], q_a[t]) for t in tiles)
-    carry = lax.fori_loop(0, kv - 1, step_a, (neg,) * 4 + (zero,) * 4 + tops + (one,))
-    values(3, vtac[kv - 2], carry[12], accs_a[3])
-    pos_k = y * new_a + lax.broadcasted_iota(jnp.int32, (new_a, rows), 0)
-    pos_q = token_of_lane((new_a, rows))
-    row = lax.broadcasted_iota(jnp.int32, (dim, tq), 0)
-    for t in tiles:
-        m, l, alpha = expo(t, carry[t], carry[4 + t], carry[8 + t])
-        values(t, vtac[kv - 1], alpha, accs_a[t])
-        s = jnp.where(pos_k <= pos_q + t * tq, qk(kan[...], q_a[t]), NEG)
-        m, l = soft_step(scale2, s, vtan[...], m, total(l), accs_a[t])
-        stat = jnp.zeros((dim, tq), jnp.float32)
-        for g in range(grp):
-            cols = slice(g * tq, (g + 1) * tq)
-            oastage[pl.ds(t * tq, tq), pl.ds(g * dim, dim)] = acc_a[t, :, cols].T
-            stat = jnp.where(row == g, m[:, cols], stat)
-            stat = jnp.where(row == grp + g, l[:, cols], stat)
-        ststage[pl.ds(t * tq, tq), :] = stat.T
-
-    def give_a(k, _):
-        yy = lax.rem(y + k, ny)
-        r = pl.ds(pl.multiple_of(yy * new_a, new_a), new_a)
-        put(OA, oastage.at[r, :], oarecv.at[y], dev(yy, x, c))
-        put(ST, ststage.at[r, :], strecv.at[y], dev(yy, x, c))
-        return 0
-
-    lax.fori_loop(1, ny, give_a, 0)
-    copy(oastage.at[row_a, :], oarecv.at[y], recv_sem.at[OA])
-    copy(ststage.at[row_a, :], strecv.at[y], recv_sem.at[ST])
 
     ring_last(2, kn)
     ring_last(3, vn)
@@ -465,36 +415,91 @@
                     o[:, g * tq:(g + 1) * tq].T.astype(bf))
         for cc in range(CORES):
             u = yy * CORES + cc
-            give(OB, obuf.at[u], ob.at[:, pl.ds(pl.multiple_of(hb * width, width), width)], peer_y(u))
+            give(OB, obuf.at[u], ob.at[:, pl.ds(pl.multiple_of(mine * width, width), width)], peer(u))
         return tuple(tops)
 
     tops = tuple(scores(t, new_keys(0), q_all[4 * row_of(1) + t]) for t in tiles)
-    tops = lax.fori_loop(0, ny - 1, rows_n, tops)
+    tops = lax.fori_loop(0, 1, rows_n, tops)
+
+    wait_in(QX, others(qabuf))
+    wait_in(KAC, kac)
+    wait_in(VAC, vac)
+    wait_in(KAN, kan)
+    wait_in(VAN, van)
+    turn(kv, vtac, lambda j: vac[j])
+    vtan[...] = van[...].T
+    for t in tiles:
+        for g in range(grp):
+            q_a[t, pl.ds(g * tq, tq), :] = qabuf[pl.ds(t * tq, tq), pl.ds(g * dim, dim)]
+    acc_a[...] = jnp.zeros_like(acc_a)
+    p3[...] = jnp.zeros_like(p3)
+    accs_a = [acc_a.at[t] for t in tiles]
+
+    def step_a(j, carry):
+        return step(carry, vtac[lax.max(j - 1, 0)], vtac[j], kac[j + 1], lambda t: q_a[t], accs_a[3], accs_a)
+
+    tops = tuple(scores(t, kac[0], q_a[t]) for t in tiles)
+    carry = lax.fori_loop(0, kv - 1, step_a, (neg,) * 4 + (zero,) * 4 + tops + (one,))
+    values(3, vtac[kv - 2], carry[12], accs_a[3])
+
+    def token_a(r, xx):
+        holder = dev(r // (CORES * ta), xx, lax.rem(r // ta, CORES))
+        return holder * ta + lax.rem(r, ta)
+
+    pos_k = token_a(lax.broadcasted_iota(jnp.int32, (new_a, rows), 0), x)
+    place_q = token_of_lane((new_a, rows))
+    row = lax.broadcasted_iota(jnp.int32, (dim, tq), 0)
+    for t in tiles:
+        m, l, alpha = expo(t, carry[t], carry[4 + t], carry[8 + t])
+        values(t, vtac[kv - 1], alpha, accs_a[t])
+        s = jnp.where(pos_k <= token_a(place_q, t), qk(kan[...], q_a[t]), NEG)
+        m, l = soft_step(scale2, s, vtan[...], m, total(l), accs_a[t])
+        stat = jnp.zeros((dim, tq), jnp.float32)
+        for g in range(grp):
+            cols = slice(g * tq, (g + 1) * tq)
+            oastage[pl.ds(t * tq, tq), pl.ds(g * dim, dim)] = acc_a[t, :, cols].T
+            stat = jnp.where(row == g, m[:, cols], stat)
+            stat = jnp.where(row == grp + g, l[:, cols], stat)
+        ststage[pl.ds(t * tq, tq), :] = stat.T
+
+    def give_a(k, _):
+        xx = lax.rem(x + k, nx)
+        r = pl.ds(pl.multiple_of(xx * new_a, new_a), new_a)
+        put(OA, oastage.at[r, :], oarecv.at[x], dev(y, xx, c))
+        put(ST, ststage.at[r, :], strecv.at[x], dev(y, xx, c))
+        return 0
+
+    lax.fori_loop(1, nx, give_a, 0)
+    copy(oastage.at[col_a, :], oarecv.at[x], recv_sem.at[OA])
+    copy(ststage.at[col_a, :], strecv.at[x], recv_sem.at[ST])
+
+    tops = tuple(scores(t, new_keys(0), q_all[4 * row_of(2) + t]) for t in tiles)
+    tops = lax.fori_loop(1, ny - 1, rows_n, tops)
 
     wait_in(OA, oarecv)
     wait_in(ST, strecv)
     for g in range(grp):
         cols = pl.ds(g * dim, dim)
-        ms = [strecv[i, :, g:g + 1] for i in range(ny)]
+        ms = [strecv[i, :, g:g + 1] for i in range(nx)]
         top = functools.reduce(jnp.maximum, ms)
         num = jnp.zeros((new_a, dim), jnp.float32)
         den = jnp.zeros((new_a, 1), jnp.float32)
-        for i in range(ny):
+        for i in range(nx):
             w = jnp.exp2((ms[i] - top) * scale2)
             num = num + w * oarecv[i, :, cols]
             den = den + w * strecv[i, :, grp + g:grp + g + 1]
         odone[:, cols] = (num / den).astype(bf)
 
     def home_a(r, _):
-        give(OX, odone.at[pl.ds(pl.multiple_of(r * ta, ta), ta), :],
-             oa.at[:, pl.ds(pl.multiple_of(ha * width, width), width)], peer_x(r))
+        give(OY, odone.at[pl.ds(pl.multiple_of(r * ta, ta), ta), :],
+             oa.at[:, pl.ds(pl.multiple_of(mine * width, width), width)], peer(r))
         return 0
 
     lax.fori_loop(0, kv, home_a, 0)
     lax.fori_loop(ny - 1, ny, rows_n, tops)
 
     wait_in(OB, ob)
-    wait_in(OX, oa)
+    wait_in(OY, oa)
     for i, ref in enumerate((nkb, nka, nvb, nva)):
         wait(ref, out_sem.at[i])
     most = pl.ds(0, kv - 1)
@@ -508,10 +513,10 @@
     for item, ref in ((KAN, kan), (VAN, van)):
         wait_out(item, ref.at[pl.ds(0, (kv - 1) * ta), :])
     wait_out(QA, qabuf.at[pl.ds(0, (kv - 1) * ta), :])
-    wait_out(OX, odone.at[pl.ds(0, (kv - 1) * ta), :])
-    wait_out(QY, other_rows(qabuf))
-    wait_out(OA, oarecv.at[pl.ds(0, ny - 1)])
-    wait_out(ST, strecv.at[pl.ds(0, ny - 1)])
+    wait_out(OY, odone.at[pl.ds(0, (kv - 1) * ta), :])
+    wait_out(QX, others(qabuf))
+    wait_out(OA, oarecv.at[pl.ds(0, nx - 1)])
+    wait_out(ST, strecv.at[pl.ds(0, nx - 1)])
     ring_drain(0, kc)
     ring_drain(1, vc)
     ring_drain(2, kn)
@@ -528,12 +533,12 @@
     rows, width = grp * tq, grp * dim
     blk = CORES * tb
     assert blk == ca and (ny * nx * CORES * cb) % (ny * blk) == 0 and (cp * ta) % (2 * tq) == 0
-    assert width == 2 * CORES * dim and cp * ta == 4 * tq and CORES == 2
+    assert width == 2 * CORES * dim and kv * ta == tq and nx == 4 and CORES == 2
     bf, f32 = jnp.bfloat16, jnp.float32
     vm = pltpu.VMEM
     scratch = [
         vm((tb + ta, model), bf),
-        vm((2, model, width), bf),
+        vm((SLOTS, model, width), bf),
         vm((kv, tb + ta, width), bf),
         vm((ny, tb + ta, width), bf),
         vm(kcb.shape, bf), vm(vcb.shape, bf), vm(kca.shape, bf), vm(vca.shape, bf),
@@ -562,14 +567,14 @@
         vm((dim, kv * ta), bf),
         vm((cp * ta, width), f32),
         vm((cp * ta, dim), f32),
-        vm((ny, kv * ta, width), f32),
-        vm((ny, kv * ta, dim), f32),
+        vm((nx, kv * ta, width), f32),
+        vm((nx, kv * ta, dim), f32),
         vm((kv * ta, width), bf),
         vm((4, dim, rows), f32),
         pltpu.SemaphoreType.DMA((15 + ny + 16,)),
         pltpu.SemaphoreType.DMA((15 + ny + 16,)),
         pltpu.SemaphoreType.DMA((5,)),
-        pltpu.SemaphoreType.DMA((2,)),
+        pltpu.SemaphoreType.DMA((SLOTS,)),
         pltpu.SemaphoreType.DMA((4,)),
     ]
     any_spec = pl.BlockSpec(memory_space=pl.ANY)
@@ -589,9 +594,6 @@
     )(xb, xa, cosf, sinf, wq, wk, wv, kcb, vcb, kca, vca)
 
 
-SLOTS = 3
-
-
 def out_kernel(ob, oa, w, kb, vb, ka, va, yb, ya, nkb, nvb, nka, nva, o, wbuf, ybuf, *rest):
     new, turned, (wsem, osem, nsem, ysem) = rest[:4], rest[4:8], rest[8:]
     tb, ta = ob.shape[0], oa.shape[0]

time: 169 us -> 165 us (0.976)
  Pallas kernels: 166 us -> 162 us
    pallas_call x1, Pallas kernels: 151 us -> 147 us  [attention(): pl.pallas_call(functools.partial(kernel, (ny, nx, kv, grp, dim)), out_sha...]
where the time goes in v5:
time: 165 us
  Pallas kernels  162 us (98%)
    pallas_call x1, Pallas kernels, attention(): pl.pallas_call(functools.partial(kernel, (ny, nx, kv, grp, dim)), out_sha...  147 us
    pallas_call x1, Pallas kernels, output_projection(): pl.pallas_call(out_kernel, out_shape=[shape((tb, model), bf), shape((ta,...  15 us

profile of v5, /device:TPU:103, one launch (start us, length us, event | category | flops | bytes accessed | tf_op | source)
XLA Modules:
  0.0 164.6 jit_solution(14384840040592130321)
XLA Ops:
  0.7 0.6 fusion
  1.3 0.9 pad_maximum_fusion
  2.1 147.3 %attend.1 = (bf16[256,4096]{1,0:T(8,128)(2,1)}, bf16[16,4096]{1,0:T(8,128)(2,1)}, bf16[8,256,128]{2,1,0:T(8,128)(2,1)}, bf16[8,256,128]{2,1,0:T(8,128)(2,1)}, bf...) custom-call(bf16[256,4096]{1,0:T(8,128)(2,1)} %xb.1, bf16[16,4096]{1,0:T(8,128)(2,1)} %xa.1, ...), custom_call_target="tpu_custom_call" | custom-call | tf_op jit(solution)/shard_map/attend/pallas_call | solution.py:583
  149.4 15.0 %project_out.1 = (bf16[256,4096]{1,0:T(8,128)(2,1)}, bf16[16,4096]{1,0:T(8,128)(2,1)}, bf16[256,8,128]{2,1,0:T(8,128)(2,1)}, bf16[256,8,128]{2,1,0:T(8,128)(2,1)...) custom-call(bf16[256,4096]{1,0:T(8,128)(2,1)} %get-tuple-element.18.ob, ...), custom_call_target="tpu_custom_call" | custom-call | tf_op jit(solution)/shard_map/project_out/pallas_call | solution.py:654
  (4 shorter events, 0.0 us)

commit v6 on v5

--- a/solution.py
+++ b/solution.py
@@ -319,11 +319,11 @@
     p3[...] = jnp.zeros_like(p3)
 
     def row_of(i):
-        return lax.rem(y + i, ny)
+        return lax.rem(y + ny - i, ny)
 
     def arrive_q(i):
         yy = row_of(i)
-        wait_in(QS + i, qbuf.at[pl.ds(yy * CORES, CORES)])
+        wait_in(QS + (ny - i) % ny, qbuf.at[pl.ds(yy * CORES, CORES)])
         for t in tiles:
             u, half = yy * CORES + t // 2, t % 2
             for g in range(grp):
@@ -379,8 +379,11 @@
     def new_keys(j):
         return kn[j // nx, lax.rem(j, nx)]
 
+    def row_n(i):
+        return lax.rem(y + ny + jnp.where(c == 0, 1 + i, ny - 1 - i), ny)
+
     def rows_n(i, tops):
-        yy, y_after = row_of(1 + i), row_of(lax.min(2 + i, ny))
+        yy, y_after = row_n(i), row_n(lax.min(i + 1, ny - 1))
         last = yy * nx + x
         accs = [acc.at[4 * yy + t] for t in tiles]
         p3[...] = jnp.zeros_like(p3)
@@ -418,7 +421,7 @@
             give(OB, obuf.at[u], ob.at[:, pl.ds(pl.multiple_of(mine * width, width), width)], peer(u))
         return tuple(tops)
 
-    tops = tuple(scores(t, new_keys(0), q_all[4 * row_of(1) + t]) for t in tiles)
+    tops = tuple(scores(t, new_keys(0), q_all[4 * row_n(0) + t]) for t in tiles)
     tops = lax.fori_loop(0, 1, rows_n, tops)
 
     wait_in(QX, others(qabuf))
@@ -473,7 +476,7 @@
     copy(oastage.at[col_a, :], oarecv.at[x], recv_sem.at[OA])
     copy(ststage.at[col_a, :], strecv.at[x], recv_sem.at[ST])
 
-    tops = tuple(scores(t, new_keys(0), q_all[4 * row_of(2) + t]) for t in tiles)
+    tops = tuple(scores(t, new_keys(0), q_all[4 * row_n(1) + t]) for t in tiles)
     tops = lax.fori_loop(1, ny - 1, rows_n, tops)
 
     wait_in(OA, oarecv)

time: 165 us -> 156 us (0.945)
  Pallas kernels: 162 us -> 154 us
    pallas_call x1, Pallas kernels: 147 us -> 139 us  [attention(): pl.pallas_call(functools.partial(kernel, (ny, nx, kv, grp, dim)), out_sha...]
where the time goes in v6:
time: 156 us
  Pallas kernels  154 us (99%)
    pallas_call x1, Pallas kernels, attention(): pl.pallas_call(functools.partial(kernel, (ny, nx, kv, grp, dim)), out_sha...  139 us
    pallas_call x1, Pallas kernels, output_projection(): pl.pallas_call(out_kernel, out_shape=[shape((tb, model), bf), shape((ta,...  15 us

profile of v6, /device:TPU:103, one launch (start us, length us, event | category | flops | bytes accessed | tf_op | source)
XLA Modules:
  0.0 156.3 jit_solution(8243717867132815820)
XLA Ops:
  0.7 0.6 fusion
  1.3 0.9 pad_maximum_fusion
  2.1 139.0 %attend.1 = (bf16[256,4096]{1,0:T(8,128)(2,1)}, bf16[16,4096]{1,0:T(8,128)(2,1)}, bf16[8,256,128]{2,1,0:T(8,128)(2,1)}, bf16[8,256,128]{2,1,0:T(8,128)(2,1)}, bf...) custom-call(bf16[256,4096]{1,0:T(8,128)(2,1)} %xb.1, bf16[16,4096]{1,0:T(8,128)(2,1)} %xa.1, ...), custom_call_target="tpu_custom_call" | custom-call | tf_op jit(solution)/shard_map/attend/pallas_call | solution.py:586
  141.1 15.0 %project_out.1 = (bf16[256,4096]{1,0:T(8,128)(2,1)}, bf16[16,4096]{1,0:T(8,128)(2,1)}, bf16[256,8,128]{2,1,0:T(8,128)(2,1)}, bf16[256,8,128]{2,1,0:T(8,128)(2,1)...) custom-call(bf16[256,4096]{1,0:T(8,128)(2,1)} %get-tuple-element.18.ob, ...), custom_call_target="tpu_custom_call" | custom-call | tf_op jit(solution)/shard_map/project_out/pallas_call | solution.py:657
  (4 shorter events, 0.0 us)

commit v7 on v6

--- a/solution.py
+++ b/solution.py
@@ -143,10 +143,14 @@
     for i in range(SLOTS - 1):
         load_cols(jnp.int32(i))
     lax.fori_loop(0, cp, greet, 0)
-    for i, (_, dst, turned) in enumerate(raw):
+
+    def turn_raw(i):
+        _, dst, turned = raw[i]
         wait(dst, load_sem.at[i])
         turned[...] = jnp.transpose(dst[...], (1, 0, 2))
-    pl.semaphore_wait(barrier, cp)
+
+    turn_raw(0)
+    turn_raw(1)
 
     def scatter(item, src, dst):
         def one(k, _):
@@ -156,10 +160,6 @@
 
         lax.fori_loop(1, kv, one, 0)
         copy(src.at[mine], dst, recv_sem.at[item])
-
-    c_rows = pl.ds(pl.multiple_of(c * cb, cb), cb)
-    scatter(KC, tkb, kc.at[y, x, c_rows, :])
-    scatter(VC, tvb, vc.at[y, x, c_rows, :])
 
     right = dev(y, lax.rem(x + 1, nx), c)
     left = dev(y, lax.rem(x + nx - 1, nx), c)
@@ -217,7 +217,7 @@
         give(QA, qsend.at[h, a_rows], qabuf.at[my_a, :], peer(h))
         return 0
 
-    def kv_step(i, _):
+    def kv_project(i):
         load_cols(i + SLOTS - 1)
         slot = lax.rem(i, SLOTS)
         wait(wbuf.at[slot], wsem.at[slot])
@@ -227,6 +227,9 @@
             cols = slice(g * dim, (g + 1) * dim)
             kvsend[p, :, cols] = rope(lin[:, cols])
         kvsend[p, :, pair:2 * pair] = lin[:, pair:2 * pair].astype(bf)
+
+    def kv_give(i):
+        p = kv_pair(i)
         for j, (nb, na) in enumerate(((nkb, nka), (nvb, nva))):
             for g in range(CORES):
                 cols = pl.ds(j * pair + g * dim, dim)
@@ -239,9 +242,19 @@
                 cols = pl.ds(j * pair + g * dim, dim)
                 give(ib, kvsend.at[p, b_rows, cols], db.at[y, x, n_rows, :], dev(p, x, g))
                 give(ia, kvsend.at[p, a_rows, cols], da.at[s_rows, :], dev(p, x, g))
+
+    def kv_step(i, _):
+        kv_project(i)
+        kv_give(i)
         return 0
 
-    lax.fori_loop(0, kv_steps, kv_step, 0)
+    kv_project(jnp.int32(0))
+    pl.semaphore_wait(barrier, cp)
+    c_rows = pl.ds(pl.multiple_of(c * cb, cb), cb)
+    scatter(KC, tkb, kc.at[y, x, c_rows, :])
+    scatter(VC, tvb, vc.at[y, x, c_rows, :])
+    kv_give(jnp.int32(0))
+    lax.fori_loop(1, kv_steps, kv_step, 0)
     wait_in(KC, kc.at[:, x])
     ring_first(0, kc)
     wait_in(VC, vc.at[:, x])
@@ -254,7 +267,9 @@
     ring_first(2, kn)
     wait_in(VN, vn.at[:, x])
     ring_first(3, vn)
+    turn_raw(2)
     scatter(KAC, tka, kac.at[mine])
+    turn_raw(3)
     scatter(VAC, tva, vac.at[mine])
 
     s_refs, p_refs = (s0, s1, s2, s3), (p0, p1, p2, p3)
@@ -304,17 +319,19 @@
     def token_of_lane(shape):
         return lax.rem(lax.broadcasted_iota(jnp.int32, shape, 1), tq)
 
-    def turn(n, dst, block):
-        def four(i, _):
-            for k in range(4):
-                dst[4 * i + k] = block(4 * i + k).T
+    def turn(first, end, dst, block):
+        n = 2 if first % 4 or end % 4 else 4
+
+        def some(i, _):
+            for k in range(n):
+                dst[n * i + k] = block(n * i + k).T
             return 0
 
-        lax.fori_loop(0, n // 4, four, 0)
+        lax.fori_loop(first // n, end // n, some, 0)
 
     blocks = vtc.shape[0]
-    per_row = blocks // ny
-    per_blk = nx // per_row
+    per_col = blocks // nx
+    part = ny // per_col
     acc[...] = jnp.zeros_like(acc)
     p3[...] = jnp.zeros_like(p3)
 
@@ -330,12 +347,16 @@
                 q_all[4 * yy + t, pl.ds(g * tq, tq), :] = qbuf[u, pl.ds(half * tq, tq), pl.ds(g * dim, dim)]
 
     def cached(buf, j):
-        return buf[j // per_row, pl.ds(lax.rem(j, per_row) * per_blk, per_blk)].reshape(blk, dim)
-
+        i = j // per_col
+        xx = jnp.where(i == 0, x, jnp.where(i == 1, x_left, jnp.where(i == 2, x_right, x_far)))
+        return buf[pl.ds(lax.rem(j, per_col) * part, part), xx].reshape(blk, dim)
+
+    def turn_c(first, end):
+        turn(first, end, vtc, lambda j: cached(vc, j))
+
+    near = blocks - per_col
     arrive_q(0)
-    ring_last(0, kc)
-    ring_last(1, vc)
-    turn(blocks, vtc, lambda j: cached(vc, j))
+    turn_c(0, near)
 
     def step_c(i, carry):
         yy, j = row_of(i // blocks), lax.rem(i, blocks)
@@ -352,9 +373,13 @@
             l_all[4 * yy + t] = out[4 + t]
         return out
 
-    tops = tuple(scores(t, cached(kc, 0), q_all[4 * y + t]) for t in tiles)
+    tops = tuple(scores(t, cached(kc, jnp.int32(0)), q_all[4 * y + t]) for t in tiles)
     carry = (neg,) * 4 + (zero,) * 4 + tops + (one,)
-    carry = lax.fori_loop(0, blocks - 1, step_c, carry)
+    carry = lax.fori_loop(0, near - 1, step_c, carry)
+    ring_last(0, kc)
+    ring_last(1, vc)
+    turn_c(near, blocks)
+    carry = lax.fori_loop(near - 1, blocks - 1, step_c, carry)
     arrive_q(1)
     carry = lax.fori_loop(blocks - 1, 2 * blocks - 1, step_c, carry)
     wait_in(QA, qabuf.at[col_a, :])
@@ -374,7 +399,7 @@
 
     ring_last(2, kn)
     ring_last(3, vn)
-    turn(ny * nx, vtn, lambda j: vn[j // nx, lax.rem(j, nx)])
+    turn(0, ny * nx, vtn, lambda j: vn[j // nx, lax.rem(j, nx)])
 
     def new_keys(j):
         return kn[j // nx, lax.rem(j, nx)]
@@ -429,7 +454,7 @@
     wait_in(VAC, vac)
     wait_in(KAN, kan)
     wait_in(VAN, van)
-    turn(kv, vtac, lambda j: vac[j])
+    turn(0, kv, vtac, lambda j: vac[j])
     vtan[...] = van[...].T
     for t in tiles:
         for g in range(grp):
@@ -535,7 +560,7 @@
     tq = tb // 2
     rows, width = grp * tq, grp * dim
     blk = CORES * tb
-    assert blk == ca and (ny * nx * CORES * cb) % (ny * blk) == 0 and (cp * ta) % (2 * tq) == 0
+    assert blk == ca and (ny * CORES * cb) % (2 * blk) == 0 and (cp * ta) % (2 * tq) == 0
     assert width == 2 * CORES * dim and kv * ta == tq and nx == 4 and CORES == 2
     bf, f32 = jnp.bfloat16, jnp.float32
     vm = pltpu.VMEM

time: 156 us -> 164 us (1.051)
  Pallas kernels: 154 us -> 161 us
    pallas_call x1, Pallas kernels: 139 us -> 146 us  [attention(): pl.pallas_call(functools.partial(kernel, (ny, nx, kv, grp, dim)), out_sha...]
where the time goes in v7:
time: 164 us
  Pallas kernels  161 us (98%)
    pallas_call x1, Pallas kernels, attention(): pl.pallas_call(functools.partial(kernel, (ny, nx, kv, grp, dim)), out_sha...  146 us
    pallas_call x1, Pallas kernels, output_projection(): pl.pallas_call(out_kernel, out_shape=[shape((tb, model), bf), shape((ta,...  15 us

profile of v7, /device:TPU:103, one launch (start us, length us, event | category | flops | bytes accessed | tf_op | source)
XLA Modules:
  0.0 163.8 jit_solution(6599439547378628391)
XLA Ops:
  0.7 0.6 fusion
  1.3 0.9 pad_maximum_fusion
  2.1 146.5 %attend.1 = (bf16[256,4096]{1,0:T(8,128)(2,1)}, bf16[16,4096]{1,0:T(8,128)(2,1)}, bf16[8,256,128]{2,1,0:T(8,128)(2,1)}, bf16[8,256,128]{2,1,0:T(8,128)(2,1)}, bf...) custom-call(bf16[256,4096]{1,0:T(8,128)(2,1)} %xb.1, bf16[16,4096]{1,0:T(8,128)(2,1)} %xa.1, ...), custom_call_target="tpu_custom_call" | custom-call | tf_op jit(solution)/shard_map/attend/pallas_call | solution.py:611
  148.6 15.0 %project_out.1 = (bf16[256,4096]{1,0:T(8,128)(2,1)}, bf16[16,4096]{1,0:T(8,128)(2,1)}, bf16[256,8,128]{2,1,0:T(8,128)(2,1)}, bf16[256,8,128]{2,1,0:T(8,128)(2,1)...) custom-call(bf16[256,4096]{1,0:T(8,128)(2,1)} %get-tuple-element.18.ob, ...), custom_call_target="tpu_custom_call" | custom-call | tf_op jit(solution)/shard_map/project_out/pallas_call | solution.py:682
  (4 shorter events, 0.0 us)

commit v8 on v7

--- a/solution.py
+++ b/solution.py
@@ -143,14 +143,10 @@
     for i in range(SLOTS - 1):
         load_cols(jnp.int32(i))
     lax.fori_loop(0, cp, greet, 0)
-
-    def turn_raw(i):
-        _, dst, turned = raw[i]
+    for i, (_, dst, turned) in enumerate(raw):
         wait(dst, load_sem.at[i])
         turned[...] = jnp.transpose(dst[...], (1, 0, 2))
-
-    turn_raw(0)
-    turn_raw(1)
+    pl.semaphore_wait(barrier, cp)
 
     def scatter(item, src, dst):
         def one(k, _):
@@ -160,6 +156,10 @@
 
         lax.fori_loop(1, kv, one, 0)
         copy(src.at[mine], dst, recv_sem.at[item])
+
+    c_rows = pl.ds(pl.multiple_of(c * cb, cb), cb)
+    scatter(KC, tkb, kc.at[y, x, c_rows, :])
+    scatter(VC, tvb, vc.at[y, x, c_rows, :])
 
     right = dev(y, lax.rem(x + 1, nx), c)
     left = dev(y, lax.rem(x + nx - 1, nx), c)
@@ -217,7 +217,7 @@
         give(QA, qsend.at[h, a_rows], qabuf.at[my_a, :], peer(h))
         return 0
 
-    def kv_project(i):
+    def kv_step(i, _):
         load_cols(i + SLOTS - 1)
         slot = lax.rem(i, SLOTS)
         wait(wbuf.at[slot], wsem.at[slot])
@@ -227,9 +227,6 @@
             cols = slice(g * dim, (g + 1) * dim)
             kvsend[p, :, cols] = rope(lin[:, cols])
         kvsend[p, :, pair:2 * pair] = lin[:, pair:2 * pair].astype(bf)
-
-    def kv_give(i):
-        p = kv_pair(i)
         for j, (nb, na) in enumerate(((nkb, nka), (nvb, nva))):
             for g in range(CORES):
                 cols = pl.ds(j * pair + g * dim, dim)
@@ -242,19 +239,9 @@
                 cols = pl.ds(j * pair + g * dim, dim)
                 give(ib, kvsend.at[p, b_rows, cols], db.at[y, x, n_rows, :], dev(p, x, g))
                 give(ia, kvsend.at[p, a_rows, cols], da.at[s_rows, :], dev(p, x, g))
-
-    def kv_step(i, _):
-        kv_project(i)
-        kv_give(i)
         return 0
 
-    kv_project(jnp.int32(0))
-    pl.semaphore_wait(barrier, cp)
-    c_rows = pl.ds(pl.multiple_of(c * cb, cb), cb)
-    scatter(KC, tkb, kc.at[y, x, c_rows, :])
-    scatter(VC, tvb, vc.at[y, x, c_rows, :])
-    kv_give(jnp.int32(0))
-    lax.fori_loop(1, kv_steps, kv_step, 0)
+    lax.fori_loop(0, kv_steps, kv_step, 0)
     wait_in(KC, kc.at[:, x])
     ring_first(0, kc)
     wait_in(VC, vc.at[:, x])
@@ -267,9 +254,7 @@
     ring_first(2, kn)
     wait_in(VN, vn.at[:, x])
     ring_first(3, vn)
-    turn_raw(2)
     scatter(KAC, tka, kac.at[mine])
-    turn_raw(3)
     scatter(VAC, tva, vac.at[mine])
 
     s_refs, p_refs = (s0, s1, s2, s3), (p0, p1, p2, p3)

time: 164 us -> 155 us (0.945)
  Pallas kernels: 161 us -> 153 us
    pallas_call x1, Pallas kernels: 146 us -> 138 us  [attention(): pl.pallas_call(functools.partial(kernel, (ny, nx, kv, grp, dim)), out_sha...]
where the time goes in v8:
time: 155 us
  Pallas kernels  153 us (99%)
    pallas_call x1, Pallas kernels, attention(): pl.pallas_call(functools.partial(kernel, (ny, nx, kv, grp, dim)), out_sha...  138 us
    pallas_call x1, Pallas kernels, output_projection(): pl.pallas_call(out_kernel, out_shape=[shape((tb, model), bf), shape((ta,...  15 us

profile of v8, /device:TPU:103, one launch (start us, length us, event | category | flops | bytes accessed | tf_op | source)
XLA Modules:
  0.0 154.9 jit_solution(793977599996676012)
XLA Ops:
  0.7 0.6 fusion
  1.3 0.9 pad_maximum_fusion
  2.1 137.6 %attend.1 = (bf16[256,4096]{1,0:T(8,128)(2,1)}, bf16[16,4096]{1,0:T(8,128)(2,1)}, bf16[8,256,128]{2,1,0:T(8,128)(2,1)}, bf16[8,256,128]{2,1,0:T(8,128)(2,1)}, bf...) custom-call(bf16[256,4096]{1,0:T(8,128)(2,1)} %xb.1, bf16[16,4096]{1,0:T(8,128)(2,1)} %xa.1, ...), custom_call_target="tpu_custom_call" | custom-call | tf_op jit(solution)/shard_map/attend/pallas_call | solution.py:596
  139.7 15.0 %project_out.1 = (bf16[256,4096]{1,0:T(8,128)(2,1)}, bf16[16,4096]{1,0:T(8,128)(2,1)}, bf16[256,8,128]{2,1,0:T(8,128)(2,1)}, bf16[256,8,128]{2,1,0:T(8,128)(2,1)...) custom-call(bf16[256,4096]{1,0:T(8,128)(2,1)} %get-tuple-element.18.ob, ...), custom_call_target="tpu_custom_call" | custom-call | tf_op jit(solution)/shard_map/project_out/pallas_call | solution.py:667
  (4 shorter events, 0.0 us)

commit v9 on v8

--- a/solution.py
+++ b/solution.py
@@ -367,18 +367,18 @@
     carry = lax.fori_loop(near - 1, blocks - 1, step_c, carry)
     arrive_q(1)
     carry = lax.fori_loop(blocks - 1, 2 * blocks - 1, step_c, carry)
-    wait_in(QA, qabuf.at[col_a, :])
-
-    def pass_qa(k, _):
-        put(QX, qabuf.at[col_a, :], qabuf.at[col_a, :], dev(y, lax.rem(x + k, nx), c))
-        return 0
-
-    lax.fori_loop(1, nx, pass_qa, 0)
     arrive_q(2)
     carry = lax.fori_loop(2 * blocks - 1, 3 * blocks - 1, step_c, carry)
     arrive_q(3)
     ring_second(2, kn)
     ring_second(3, vn)
+    wait_in(QA, qabuf.at[col_a, :])
+
+    def pass_qa(k, _):
+        put(QX, qabuf.at[col_a, :], qabuf.at[col_a, :], dev(y, lax.rem(x + k, nx), c))
+        return 0
+
+    lax.fori_loop(1, nx, pass_qa, 0)
     carry = lax.fori_loop(3 * blocks - 1, 4 * blocks, step_c, carry)
     values(3, vtc[blocks - 1], carry[12], acc.at[4 * row_of(ny - 1) + 3])
 

time: 155 us -> 156 us (level)
  no operation moved by 1% of the time
where the time goes in v9:
time: 156 us
  Pallas kernels  154 us (99%)
    pallas_call x1, Pallas kernels, attention(): pl.pallas_call(functools.partial(kernel, (ny, nx, kv, grp, dim)), out_sha...  139 us
    pallas_call x1, Pallas kernels, output_projection(): pl.pallas_call(out_kernel, out_shape=[shape((tb, model), bf), shape((ta,...  15 us

profile of v9, /device:TPU:103, one launch (start us, length us, event | category | flops | bytes accessed | tf_op | source)
XLA Modules:
  0.0 155.9 jit_solution(13158635283896123093)
XLA Ops:
  0.7 0.6 fusion
  1.3 0.9 pad_maximum_fusion
  2.1 138.6 %attend.1 = (bf16[256,4096]{1,0:T(8,128)(2,1)}, bf16[16,4096]{1,0:T(8,128)(2,1)}, bf16[8,256,128]{2,1,0:T(8,128)(2,1)}, bf16[8,256,128]{2,1,0:T(8,128)(2,1)}, bf...) custom-call(bf16[256,4096]{1,0:T(8,128)(2,1)} %xb.1, bf16[16,4096]{1,0:T(8,128)(2,1)} %xa.1, ...), custom_call_target="tpu_custom_call" | custom-call | tf_op jit(solution)/shard_map/attend/pallas_call | solution.py:596
  140.7 15.0 %project_out.1 = (bf16[256,4096]{1,0:T(8,128)(2,1)}, bf16[16,4096]{1,0:T(8,128)(2,1)}, bf16[256,8,128]{2,1,0:T(8,128)(2,1)}, bf16[256,8,128]{2,1,0:T(8,128)(2,1)...) custom-call(bf16[256,4096]{1,0:T(8,128)(2,1)} %get-tuple-element.18.ob, ...), custom_call_target="tpu_custom_call" | custom-call | tf_op jit(solution)/shard_map/project_out/pallas_call | solution.py:667
  (4 shorter events, 0.0 us)
